TPU v7x, 128 devices: a whole 4x4x4 slice. The times are simulated.
128 devices in a mesh: up: 16 (over y_lo, x, core), dn: 8 (over y_hi, z).
Axes of the slice: x: 4, y: 4 (y_hi: 2, y_lo: 2; y = y_hi * 2 + y_lo), z: 4, core: 2. Of those that a mesh axis runs over, the one named last changes fastest.
Arguments:
- start_vector: bfloat16 [13312, 13312], P('up', 'dn'), may hold values from -6 to 6
- hop_tiles: bfloat16 [104, 5, 128, 128], replicated, may hold values from -0.5 to 0.5
- tile_columns: int32 [104, 5], replicated, may hold values from 0 to 103, as said below
- tile_signs: int32 [104, 5], replicated, may hold values from 0 to 1
- occupation: int32 [16, 13312], replicated, may hold values from 0 to 1, as said below
Outputs:
- next_vector: bfloat16 [13312, 13312], P('up', 'dn')
- alphas: float32 [2], replicated
- betas: float32 [2], replicated
Inputs may be any that keep to these rules, and one draw needn't show every extreme that they name: Each row of tile_columns names 5 different tile columns. Every column of occupation holds exactly 8 ones.
All inputs are finite; a program needn't handle non-finite values.
Results may differ from a plain program's by a relative error of at most 0.0065.
Values may be sent and summed in bfloat16 or wider, within the bound.
A program may use at most 192 MiB of HBM per device.

v0:
```python
import functools

import jax
import jax.numpy as jnp
from jax import lax
from jax.experimental import pallas as pl
from jax.experimental.pallas import tpu as pltpu
from jax.sharding import PartitionSpec as P

STEPS = 2


coupling = 4.0


def hop_kernel(tile_k, tile, group, parts_tiles, columns_ref, x_ref, tiles_ref, out_ref):
    first = pl.program_id(0) * group

    def one_tile(t, carry):
        picked = []
        for k in range(tile_k):
            column = columns_ref[(first + t) * tile_k + k]
            at = pl.multiple_of(lax.rem(column, parts_tiles) * tile, tile)
            picked.append(x_ref[lax.div(column, parts_tiles), :, pl.ds(at, tile)])
        left = jnp.concatenate(picked, axis=1)
        result = jnp.dot(left, tiles_ref[t], preferred_element_type=jnp.float32)
        out_ref[0, :, pl.ds(pl.multiple_of(t * tile, tile), tile)] = result.astype(jnp.bfloat16)
        return carry

    lax.fori_loop(0, group, one_tile, 0)


def hop_blocks(x, stacked, columns, tile_k):
    parts, rows, width = x.shape
    tiles, depth, tile = stacked.shape
    if width % tile:
        joined = x.transpose(1, 0, 2).reshape(1, rows, parts * width)
        hopped = hop_blocks(joined, stacked, columns, tile_k)
        return hopped.reshape(rows, parts, width).transpose(1, 0, 2)
    parts_tiles = width // tile
    group = max(d for d in range(1, 17) if parts_tiles % d == 0)
    per_part = parts_tiles // group
    return pl.pallas_call(
        functools.partial(hop_kernel, tile_k, tile, group, parts_tiles),
        grid_spec=pltpu.PrefetchScalarGridSpec(
            num_scalar_prefetch=1,
            grid=(tiles // group,),
            in_specs=[
                pl.BlockSpec((parts, rows, width), lambda i, c: (0, 0, 0)),
                pl.BlockSpec((group, depth, tile), lambda i, c: (i, 0, 0)),
            ],
            out_specs=pl.BlockSpec(
                (1, rows, group * tile), lambda i, c: (i // per_part, 0, i % per_part)
            ),
        ),
        out_shape=jax.ShapeDtypeStruct(x.shape, jnp.bfloat16),
        compiler_params=pltpu.CompilerParams(vmem_limit_bytes=56 * 1024 * 1024),
        cost_estimate=pl.CostEstimate(
            flops=2 * rows * tiles * depth * tile,
            bytes_accessed=4 * rows * parts * width + 2 * tiles * depth * tile,
            transcendentals=0,
        ),
    )(columns, x, stacked)


def body(start_vector, hop_tiles, tile_columns, tile_signs, occupation):
    tiles, tile_k, tile, _ = hop_tiles.shape
    signed = hop_tiles * (1 - 2 * tile_signs).astype(jnp.bfloat16)[:, :, None, None]
    stacked = signed.transpose(0, 1, 3, 2).reshape(tiles, tile_k * tile, tile)
    columns = tile_columns.reshape(-1)
    block_rows, block_cols = start_vector.shape
    count_up = lax.axis_size("up")
    count_down = lax.axis_size("dn")
    row_start = lax.axis_index("up") * block_rows
    col_start = lax.axis_index("dn") * block_cols
    occ_rows = lax.dynamic_slice_in_dim(occupation, row_start, block_rows, 1).astype(jnp.bfloat16)
    occ_cols = lax.dynamic_slice_in_dim(occupation, col_start, block_cols, 1).astype(jnp.bfloat16)
    diagonal = (
        coupling * jnp.einsum("sa,sb->ab", occ_rows, occ_cols, preferred_element_type=jnp.float32)
    ).astype(jnp.bfloat16)
    total = lax.psum(jnp.sum(jnp.square(start_vector.astype(jnp.float32))), ("up", "dn"))
    scale = 1.0 / jnp.maximum(jnp.sqrt(total), 1.0)
    vector = start_vector.astype(jnp.float32) * scale
    length = total / jnp.maximum(total, 1.0)
    previous = None
    beta_value = None
    alpha_list = []
    beta_list = []
    for iteration in range(STEPS):
        rounded = start_vector if iteration == 0 else vector.astype(jnp.bfloat16)
        down = rounded.reshape(count_down, block_rows // count_down, block_cols)
        up = rounded.T.reshape(count_up, block_cols // count_up, block_rows)
        down = lax.all_to_all(down, "dn", 0, 0, tiled=True)
        up = lax.all_to_all(up, "up", 0, 0, tiled=True)
        down = hop_blocks(down, stacked, columns, tile_k)
        down = lax.all_to_all(down, "dn", 0, 0, tiled=True)
        up = hop_blocks(up, stacked, columns, tile_k)
        up = lax.all_to_all(up, "up", 0, 0, tiled=True)
        hopped_down = down.reshape(block_rows, block_cols)
        hopped_up = up.reshape(block_cols, block_rows).T
        hopped = hopped_up.astype(jnp.float32) + hopped_down.astype(jnp.float32)
        if iteration == 0:
            work = hopped * scale + diagonal * vector
        else:
            work = hopped + diagonal * vector - beta_value * previous
        intersect, square = lax.psum((jnp.sum(work * vector), jnp.sum(work * work)), ("up", "dn"))
        work = work - intersect * vector
        residual = square - 2.0 * intersect * intersect + intersect * intersect * length
        beta_value = jnp.sqrt(jnp.maximum(residual, 1.0))
        length = residual / jnp.maximum(residual, 1.0)
        previous = vector
        vector = work / beta_value
        alpha_list.append(intersect)
        beta_list.append(beta_value)
    final = vector.astype(jnp.bfloat16)
    return (final, jnp.stack(alpha_list), jnp.stack(beta_list))


def solution(mesh):
    placed = (P("up", "dn"), P(), P(), P(), P())
    return jax.shard_map(
        body, mesh=mesh, in_specs=placed, out_specs=(P("up", "dn"), P(), P()), check_vma=False
    )
```

profile of v0, /device:TPU:1, one launch (start us, length us, event | category | flops | bytes accessed | tf_op | source)
XLA Modules:
  0.0 630.0 jit_solution(464300119553604156)
XLA Ops:
  0.6 5.3 copy.15
  5.9 42.9 %all_to_all.40 = bf16[16,104,832]{2,1,0:T(8,128)(2,1)S(1)} all-to-all(bf16[16,104,832]{2,1,0:T(8,128)(2,1)} %bitcast.62), channel_id=1, replica_groups=mesh['up'=16,'dn'=8] {'up'}, dimensions={0} | all-to-all | bytes 5537792 | tf_op jit(solution)/shard_map/all_to_all | solution.py:94
  48.9 7.4 %all-to-all-start.2 = ((bf16[8,104,1664]{2,1,0:T(8,128)(2,1)}), bf16[8,104,1664]{2,1,0:T(8,128)(2,1)}, u32[]{:S(2)}, u32[]{:S(2)}) async-start(bf16[8,104,1664]{2,1,0:T(8,128)(2,1)} %bitcast.8), calls=%async_computation.2 | async-start | bytes 5537792 | tf_op jit(solution)/shard_map/all_to_all | solution.py:93
  56.2 0.0 copy-done.2
  56.2 0.1 copy.14
  56.4 0.8 reshape.49.columns_ref
  57.1 0.0 copy-done.3
  57.1 0.1 copy.17
  57.3 14.1 %multiply_bitcast_fusion = bf16[104,5,128,128]{2,3,1,0:T(8,128)(2,1)} fusion(bf16[104,5,128,128]{3,2,1,0:T(8,128)(2,1)} %param.6, bf16[104,5]{1,0:T(8,128)(2,1)S(1)} %copy.17), kind=kLoop, calls=%fused_computation | loop fusion | flops 8519680 | bytes 34079760 | tf_op jit(solution)/shard_map/transpose | solution.py:69
  71.4 22.8 %copy.18 = bf16[104,5,128,128]{3,2,1,0:T(8,128)(2,1)} copy(bf16[104,5,128,128]{2,3,1,0:T(8,128)(2,1)} %multiply_bitcast_fusion) | data formatting | bytes 34078720 | tf_op jit(solution)/shard_map/transpose | solution.py:69
  94.2 2.0 copy.16
  96.2 5.9 reshape.51.x_ref
  102.1 24.7 %shard_map.76 = bf16[1,104,13312]{2,1,0:T(8,128)(2,1)} custom-call(s32[520]{0:T(1024)} %reshape.49.columns_ref, bf16[1,104,13312]{2,1,0:T(8,128)(2,1)} %reshape.51.x_ref, bf16[104,640,128]{2,1,0:T(8,128)(2,1)} %bitcast.54), custom_call_target="tpu_custom_call" | custom-call | flops 1772093440 | bytes 22577152 | tf_op jit(solution)/shard_map/pallas_call | solution.py:43
  126.8 4.7 reshape.53
  131.5 2.2 copy.28
  133.7 0.0 all-to-all-done.2.x_ref
  133.7 4.8 all-to-all-start.1
  138.5 24.2 %shard_map.77 = bf16[8,104,1664]{2,1,0:T(8,128)(2,1)} custom-call(s32[520]{0:T(1024)} %reshape.49.columns_ref, bf16[8,104,1664]{2,1,0:T(8,128)(2,1)} %all-to-all-done.2.x_ref, bf16[104,640,128]{2,1,0:T(8,128)(2,1)} %bitcast.55), custom_call_target="tpu_custom_call" | custom-call | flops 1772093440 | bytes 22577152 | tf_op jit(solution)/shard_map/pallas_call | solution.py:43
  162.7 15.1 %all-to-all-done.1 = bf16[16,104,832]{2,1,0:T(8,128)(2,1)S(1)} async-done(((bf16[16,104,832]{2,1,0:T(8,128)(2,1)}), bf16[16,104,832]{2,1,0:T(8,128)(2,1)S(1)}, u32[]{:S(2)}, u32[]{:S(2)}) %all-to-all-start.1) | async-done | bytes 2768928 | tf_op jit(solution)/shard_map/all_to_all | solution.py:98
  177.8 6.9 %all-to-all-start.3 = ((bf16[8,104,1664]{2,1,0:T(8,128)(2,1)}), bf16[8,104,1664]{2,1,0:T(8,128)(2,1)}, u32[]{:S(2)}, u32[]{:S(2)}) async-start(bf16[8,104,1664]{2,1,0:T(8,128)(2,1)} %shard_map.77), calls=%async_computation.3 | async-start | bytes 5537792 | tf_op jit(solution)/shard_map/all_to_all | solution.py:96
  184.7 3.8 fusion.7
  188.5 85.3 %psum.35 = f32[]{:T(128)} all-reduce(f32[]{:T(128)} %fusion.7), channel_id=1, replica_groups=mesh['up'=16,'dn'=8] {'up','dn'}, use_global_device_ids=true, to_apply=%region_1.0 | all-reduce | flops 1 | bytes 8 | tf_op jit(solution)/shard_map/psum | solution.py:81
  275.9 3.2 bitcast_convert_fusion.1
  279.0 7.0 %copy.20 = f32[1664,832]{0,1:T(8,128)} copy(f32[1664,832]{1,0:T(8,128)} %bitcast_convert_fusion.1) | data formatting | bytes 11075584 | tf_op jit(solution)/shard_map/convert_element_type | solution.py:101
  286.0 0.0 all-to-all-done.3
  286.0 7.5 %fusion.3 = (f32[]{:T(128)}, f32[]{:T(128)}, bf16[832,1664]{1,0:T(8,128)(2,1)S(1)}) fusion(bf16[832,1664]{1,0:T(8,128)(2,1)} %param.5, f32[]{:T(128)S(6)} %div.21, bf16[8,104,1664]{2,1,0:T(8,128)(2,1)} %all-to-all-done.3, f32[1664,832]{0,1:T(8,128)} %copy.20, s32[16,13312]{1,0:T(8,128)} %param.9, s32[]{:T(128)S(6)} %select_n.7, s32[]{:T(128)S(6)} %select_n.6), kind=kOutput, calls=%fused_computation.8 | convolution fusion | flops 63724544 | bytes 14008340 | tf_op jit(solution)/shard_map/sa,sb->ab/dot_general | solution.py:79
  293.5 64.3 %all-reduce.1 = (f32[]{:T(128)}, f32[]{:T(128)}) all-reduce(f32[]{:T(128)} %get-tuple-element.4, f32[]{:T(128)} %get-tuple-element.3), channel_id=1, replica_groups=mesh['up'=16,'dn'=8] {'up','dn'}, use_global_device_ids=true, to_apply=%region_5.0 | all-reduce | flops 2 | bytes 16 | tf_op jit(solution)/shard_map/psum | solution.py:106
  361.1 7.9 %fusion.13 = (bf16[832,1664]{1,0:T(8,128)(2,1)}, f32[832,1664]{1,0:T(8,128)}) fusion(f32[]{:T(128)} %sqrt.10, f32[]{:T(128)} %get-tuple-element.10, bf16[832,1664]{1,0:T(8,128)(2,1)} %param.5, bf16[832,1664]{1,0:T(8,128)(2,1)S(1)} %get-tuple-element.14, f32[]{:T(128)S(6)} %div.21, bf16[8,104,1664]{2,1,0:T(8,128)(2,1)} %all-to-all-done.3, f32[1664,832]{0,1:T(8,128)} %copy.20), kind=kLoop, calls=%fused_computation.33 | loop fusion | flops 16613376 | bytes 22151180 | tf_op jit(solution)/shard_map/convert_element_type | solution.py:90
  369.0 5.3 copy.21
  374.4 40.7 %all_to_all.41 = bf16[16,104,832]{2,1,0:T(8,128)(2,1)S(1)} all-to-all(bf16[16,104,832]{2,1,0:T(8,128)(2,1)} %bitcast.63), channel_id=1, replica_groups=mesh['up'=16,'dn'=8] {'up'}, dimensions={0} | all-to-all | bytes 5537792 | tf_op jit(solution)/shard_map/all_to_all | solution.py:94
  415.0 4.4 all-to-all-start.6
  419.5 2.0 copy.22
  421.4 5.9 reshape.56.x_ref
  427.3 24.7 %shard_map.78 = bf16[1,104,13312]{2,1,0:T(8,128)(2,1)} custom-call(s32[520]{0:T(1024)} %reshape.49.columns_ref, bf16[1,104,13312]{2,1,0:T(8,128)(2,1)} %reshape.56.x_ref, bf16[104,640,128]{2,1,0:T(8,128)(2,1)} %bitcast.56), custom_call_target="tpu_custom_call" | custom-call | flops 1772093440 | bytes 22577152 | tf_op jit(solution)/shard_map/pallas_call | solution.py:43
  452.1 4.7 reshape.57
  456.8 2.2 copy.27
  458.9 0.0 all-to-all-done.6.x_ref
  459.0 4.6 all-to-all-start.5
  463.5 24.2 %shard_map.79 = bf16[8,104,1664]{2,1,0:T(8,128)(2,1)} custom-call(s32[520]{0:T(1024)} %reshape.49.columns_ref, bf16[8,104,1664]{2,1,0:T(8,128)(2,1)} %all-to-all-done.6.x_ref, bf16[104,640,128]{2,1,0:T(8,128)(2,1)} %bitcast.57), custom_call_target="tpu_custom_call" | custom-call | flops 1772093440 | bytes 22577152 | tf_op jit(solution)/shard_map/pallas_call | solution.py:43
  487.7 15.1 %all-to-all-done.5 = bf16[16,104,832]{2,1,0:T(8,128)(2,1)S(1)} async-done(((bf16[16,104,832]{2,1,0:T(8,128)(2,1)}), bf16[16,104,832]{2,1,0:T(8,128)(2,1)S(1)}, u32[]{:S(2)}, u32[]{:S(2)}) %all-to-all-start.5) | async-done | bytes 2768928 | tf_op jit(solution)/shard_map/all_to_all | solution.py:98
  502.8 6.8 %all-to-all-start.7 = ((bf16[8,104,1664]{2,1,0:T(8,128)(2,1)}), bf16[8,104,1664]{2,1,0:T(8,128)(2,1)}, u32[]{:S(2)}, u32[]{:S(2)}) async-start(bf16[8,104,1664]{2,1,0:T(8,128)(2,1)} %shard_map.79), calls=%async_computation.7 | async-start | bytes 5537792 | tf_op jit(solution)/shard_map/all_to_all | solution.py:96
  509.7 3.2 bitcast_convert_fusion
  512.8 7.2 %copy.24 = f32[1664,832]{0,1:T(8,128)} copy(f32[1664,832]{1,0:T(8,128)} %bitcast_convert_fusion) | data formatting | bytes 11075584 | tf_op jit(solution)/shard_map/convert_element_type | solution.py:101
  520.0 23.1 %all-to-all-done.7 = bf16[8,104,1664]{2,1,0:T(8,128)(2,1)} async-done(((bf16[8,104,1664]{2,1,0:T(8,128)(2,1)}), bf16[8,104,1664]{2,1,0:T(8,128)(2,1)}, u32[]{:S(2)}, u32[]{:S(2)}) %all-to-all-start.7) | async-done | bytes 2768928 | tf_op jit(solution)/shard_map/all_to_all | solution.py:96
  543.2 9.7 %multiply_reduce_fusion.1 = (f32[]{:T(128)}, f32[]{:T(128)}, f32[832,1664]{1,0:T(8,128)}) fusion(f32[832,1664]{1,0:T(8,128)} %get-tuple-element.13, f32[]{:T(128)S(6)} %div.21, bf16[832,1664]{1,0:T(8,128)(2,1)} %param.5, f32[]{:T(128)} %sqrt.10, bf16[832,1664]{1,0:T(8,128)(2,1)S(1)} %copy-done.1, bf16[8,104,1664]{2,1,0:T(8,128)(2,1)} %all-to-all-done.7, ...), kind=kLoop, calls=%fused_computation.20 | loop fusion | flops 17997822 | bytes 24920080 | tf_op jit(solution)/shard_map/reduce_sum | solution.py:106
  552.8 65.0 %all-reduce = (f32[]{:T(128)}, f32[]{:T(128)}) all-reduce(f32[]{:T(128)} %get-tuple-element.6, f32[]{:T(128)} %get-tuple-element.5), channel_id=1, replica_groups=mesh['up'=16,'dn'=8] {'up','dn'}, use_global_device_ids=true, to_apply=%region_9.0 | all-reduce | flops 2 | bytes 16 | tf_op jit(solution)/shard_map/psum | solution.py:106
  621.0 7.1 %divide_convert_fusion = bf16[832,1664]{1,0:T(8,128)(2,1)} fusion(f32[832,1664]{1,0:T(8,128)} %get-tuple-element.11, f32[832,1664]{1,0:T(8,128)} %get-tuple-element.13, f32[]{:T(128)} %sqrt.11, f32[]{:T(128)} %get-tuple-element.8), kind=kLoop, calls=%fused_computation.18 | loop fusion | flops 5537792 | bytes 13844488 | tf_op jit(solution)/shard_map/convert_element_type | solution.py:115
  628.1 1.8 pad_maximum_fusion
  (7 shorter events, 0.0 us)
Async XLA Ops:
  5.9 50.3 %copy-start.2 = (s32[104,5]{0,1:T(8,128)S(1)}, s32[104,5]{0,1:T(8,128)}, u32[]{:S(2)}) copy-start(s32[104,5]{0,1:T(8,128)} %param.7) | copy-start | bytes 6244
  5.9 51.2 %copy-start.3 = (s32[104,5]{0,1:T(8,128)S(1)}, s32[104,5]{0,1:T(8,128)}, u32[]{:S(2)}) copy-start(s32[104,5]{0,1:T(8,128)} %param.8) | copy-start | bytes 6244
  48.9 84.8 %all-to-all-start.2 = ((bf16[8,104,1664]{2,1,0:T(8,128)(2,1)}), bf16[8,104,1664]{2,1,0:T(8,128)(2,1)}, u32[]{:S(2)}, u32[]{:S(2)}) async-start(bf16[8,104,1664]{2,1,0:T(8,128)(2,1)} %bitcast.8), calls=%async_computation.2 | async-start | bytes 5537792 | tf_op jit(solution)/shard_map/all_to_all | solution.py:93
  133.7 44.1 %all-to-all-start.1 = ((bf16[16,104,832]{2,1,0:T(8,128)(2,1)}), bf16[16,104,832]{2,1,0:T(8,128)(2,1)S(1)}, u32[]{:S(2)}, u32[]{:S(2)}) async-start(bf16[16,104,832]{2,1,0:T(8,128)(2,1)} %bitcast.60), calls=%async_computation.1 | async-start | bytes 5963776 | tf_op jit(solution)/shard_map/all_to_all | solution.py:98
  177.8 108.2 %all-to-all-start.3 = ((bf16[8,104,1664]{2,1,0:T(8,128)(2,1)}), bf16[8,104,1664]{2,1,0:T(8,128)(2,1)}, u32[]{:S(2)}, u32[]{:S(2)}) async-start(bf16[8,104,1664]{2,1,0:T(8,128)(2,1)} %shard_map.77), calls=%async_computation.3 | async-start | bytes 5537792 | tf_op jit(solution)/shard_map/all_to_all | solution.py:96
  293.5 75.5 %copy-start = (bf16[832,1664]{1,0:T(8,128)(2,1)}, bf16[832,1664]{1,0:T(8,128)(2,1)S(1)}, u32[]{:S(2)}) copy-start(bf16[832,1664]{1,0:T(8,128)(2,1)S(1)} %get-tuple-element.14) | copy-start | bytes 8306692
  415.0 43.9 %all-to-all-start.6 = ((bf16[8,104,1664]{2,1,0:T(8,128)(2,1)}), bf16[8,104,1664]{2,1,0:T(8,128)(2,1)}, u32[]{:S(2)}, u32[]{:S(2)}) async-start(bf16[8,104,1664]{2,1,0:T(8,128)(2,1)} %bitcast.16), calls=%async_computation.6 | async-start | bytes 5537792 | tf_op jit(solution)/shard_map/all_to_all | solution.py:93
  459.0 43.9 %all-to-all-start.5 = ((bf16[16,104,832]{2,1,0:T(8,128)(2,1)}), bf16[16,104,832]{2,1,0:T(8,128)(2,1)S(1)}, u32[]{:S(2)}, u32[]{:S(2)}) async-start(bf16[16,104,832]{2,1,0:T(8,128)(2,1)} %bitcast.59), calls=%async_computation.5 | async-start | bytes 5963776 | tf_op jit(solution)/shard_map/all_to_all | solution.py:98
  502.8 40.3 %all-to-all-start.7 = ((bf16[8,104,1664]{2,1,0:T(8,128)(2,1)}), bf16[8,104,1664]{2,1,0:T(8,128)(2,1)}, u32[]{:S(2)}, u32[]{:S(2)}) async-start(bf16[8,104,1664]{2,1,0:T(8,128)(2,1)} %shard_map.79), calls=%async_computation.7 | async-start | bytes 5537792 | tf_op jit(solution)/shard_map/all_to_all | solution.py:96
  512.8 30.3 %copy-start.1 = (bf16[832,1664]{1,0:T(8,128)(2,1)S(1)}, bf16[832,1664]{1,0:T(8,128)(2,1)}, u32[]{:S(2)}) copy-start(bf16[832,1664]{1,0:T(8,128)(2,1)} %copy-done) | copy-start | bytes 8306692
where the time goes:
time: 633 us; the launch traced here: 630 us
  blocking collectives  298 us (47%)
  Pallas kernels  97.9 us (15%)
  local copies, waits for them, and re-layouts  78.1 us (12%)
  waiting for transfers between devices  53.3 us (8%)
  other arithmetic  50.9 us (8%)
  starting transfers between devices  35 us (6%)
  between operations  9.17 us (1%)
  matrix products  7.5 us (1%)
    psum x2, blocking collectives, body(): lax.psum((jnp.sum(work * vector), jnp.sum(work * work)), ('up', 'dn'))  129 us
    pallas_call x4, Pallas kernels, hop_blocks(): pl.pallas_call(functools.partial(hop_kernel, tile_k, tile, group, parts_t...  97.9 us
    psum x1, blocking collectives, body(): lax.psum(jnp.sum(jnp.square(start_vector.astype(jnp.float32))), ('up', 'd...  85.3 us
    all_to_all x2, blocking collectives, body(): up = lax.all_to_all(up, 'up', 0, 0, tiled=True)  83.6 us
    all_to_all x2, waiting for transfers between devices, body(): up = lax.all_to_all(up, 'up', 0, 0, tiled=True)  30.2 us
    all_to_all x4, starting transfers between devices, body(): down = lax.all_to_all(down, 'dn', 0, 0, tiled=True)  25.5 us
    all_to_all x4, waiting for transfers between devices, body(): down = lax.all_to_all(down, 'dn', 0, 0, tiled=True)  23.1 us
    transpose x1, local copies, waits for them, and re-layouts, body(): stacked = signed.transpose(0, 1, 3, 2).reshape(tiles, tile_k * tile, tile)  22.8 us
  transfers between devices with their start and end apart: 6, of which 3 were waited for; matrix products, arithmetic and copies ran while one was open for 15% of the time, Pallas kernels for 16%

commit v1 on v0

v1 whole, which is shorter than its diff:
```python
import functools

import jax
import jax.numpy as jnp
from jax import lax
from jax.experimental import pallas as pl
from jax.experimental.pallas import tpu as pltpu
from jax.sharding import PartitionSpec as P

STEPS = 2
RING = 4
TILE = 128
MESH = pl.DeviceIdType.MESH

coupling = 4.0


def place():
    u = lax.axis_index("up")
    d = lax.axis_index("dn")
    return u // 8, (u // 2) % 4, u % 2, d // 4, d % 4


def device(y_lo, x, core, y_hi, z):
    return (y_lo * 8 + x * 2 + core, y_hi * 4 + z)


def turn(source, target, side):
    tiles = side // TILE

    def one_row(i, carry):
        at = pl.multiple_of(i * TILE, TILE)
        for j in range(tiles):
            target[i, j * TILE : (j + 1) * TILE, :] = source[j, pl.ds(at, TILE), :].T
        return carry

    lax.fori_loop(0, tiles, one_row, 0)


def exchange_kernel(
    tile_k,
    columns_ref,
    signs_ref,
    x_ref,
    tiles_ref,
    mine_ref,
    other_ref,
    own,
    near,
    far,
    turned,
    turned_near,
    gathered,
    result,
    returned,
    weights,
    load_sem,
    tiles_sem,
    sib_send,
    sib_recv,
    near_send,
    near_recv,
    far_send,
    far_recv,
    share_send,
    share_recv,
    ring_send,
    ring_recv,
    back_send,
    back_recv,
    last_send,
    last_recv,
):
    half = x_ref.shape[0]
    side = 2 * half
    quarter = side // RING
    chunks = near_send.shape[0]
    step = half // chunks
    per_piece = side // TILE
    held = RING * per_piece
    y_lo, x, core, y_hi, z = place()
    r = z + core * (x - z)
    h = y_hi + core * (y_lo - y_hi)
    sibling = device(y_lo, x, 1 - core, y_hi, z)
    near_chip = device(1 - y_lo, x, core, y_hi, z)
    far_chip = device(1 - y_lo, x, core, 1 - y_hi, z)

    def ring_peer(p):
        return device(y_lo, x + core * (p - x), core, y_hi, p + core * (z - p))

    def remote(src, dst, send, recv, to):
        return pltpu.make_async_remote_copy(
            src_ref=src, dst_ref=dst, send_sem=send, recv_sem=recv, device_id=to, device_id_type=MESH
        )

    barrier = pltpu.get_barrier_semaphore()
    greeted = [sibling, near_chip, far_chip] + [ring_peer((r + k) % RING) for k in range(1, RING)]
    for to in greeted:
        pl.semaphore_signal(barrier, inc=1, device_id=to, device_id_type=MESH)
    pl.semaphore_wait(barrier, len(greeted))

    base = pl.multiple_of(core * half, half)
    my_half = pl.ds(base, half)
    loads = []
    for t in range(per_piece):
        copy = pltpu.make_async_copy(
            x_ref.at[:, pl.ds(t * TILE, TILE)], own.at[t, my_half], load_sem.at[t]
        )
        copy.start()
        loads.append(copy)
    for copy in loads:
        copy.wait()
    to_sibling = remote(own.at[:, my_half], own.at[:, my_half], sib_send, sib_recv, sibling)
    to_sibling.start()
    to_near = []
    for q in range(chunks):
        rows = pl.ds(pl.multiple_of(base + q * step, step), step)
        copy = remote(
            own.at[:, rows], near.at[:, rows], near_send.at[q], near_recv.at[q], near_chip
        )
        copy.start()
        to_near.append(copy)
    first = pl.multiple_of(h * held, held)
    load_tiles = pltpu.make_async_copy(tiles_ref.at[pl.ds(first, held)], weights, tiles_sem)
    load_tiles.start()
    to_sibling.wait_recv()

    def ring_out(block, slot, which):
        copies = []
        for k in (2, 1, 3):
            p = (r + k) % RING
            rows = pl.ds(pl.multiple_of(p * quarter, quarter), quarter)
            copy = remote(
                block.at[:, rows], gathered.at[slot], ring_send.at[which, k - 1], ring_recv.at[which, k - 1], ring_peer(p)
            )
            copy.start()
            copies.append(copy)
        rows = pl.ds(pl.multiple_of(r * quarter, quarter), quarter)
        gathered[slot] = block[:, rows]
        return copies

    own_slot = pl.ds((h * RING + r) * per_piece, per_piece)
    near_slot = pl.ds(((1 - h) * RING + r) * per_piece, per_piece)

    def ring_copies(block, slot, which):
        for k in range(1, RING):
            p = (r + k) % RING
            rows = pl.ds(pl.multiple_of(p * quarter, quarter), quarter)
            remote(
                block.at[:, rows], gathered.at[slot], ring_send.at[which, k - 1], ring_recv.at[which, k - 1], ring_peer(p)
            ).wait()

    @pl.when(core == 0)
    def _():
        ring_out(own, own_slot, 0)

    @pl.when(core == 1)
    def _():
        turn(own, turned, side)
        ring_out(turned, own_slot, 0)

    def chunk_rows(of, q):
        return pl.ds(of * half + q * step, step)

    def forward(q):
        rows = pl.ds(pl.multiple_of(base + q * step, step), step)
        return remote(near.at[:, rows], far.at[:, rows], far_send.at[q], far_recv.at[q], far_chip)

    def share_near(q):
        rows = chunk_rows(0, q)
        return remote(near.at[:, rows], near.at[:, rows], share_send.at[q], share_recv.at[q], sibling)

    def share_far(q):
        rows = chunk_rows(1, q)
        return remote(far.at[:, rows], far.at[:, rows], share_send.at[q], share_recv.at[q], sibling)

    for q in range(chunks):
        to_near[q].wait_recv()
        forward(q).start()

        @pl.when(core == 0)
        def _():
            share_near(q).start()

    @pl.when(core == 0)
    def _():
        for q in range(chunks):
            forward(q).wait_recv()
        for q in range(chunks):
            share_far(q).wait_recv()
        ring_out(far, near_slot, 1)

    @pl.when(core == 1)
    def _():
        for q in range(chunks):
            share_near(q).wait_recv()
        turn(near, turned_near, side)
        ring_out(turned_near, near_slot, 1)
        for q in range(chunks):
            forward(q).wait_recv()
            share_far(q).start()

    load_tiles.wait()
    ring_copies(own, own_slot, 0)
    ring_copies(far, near_slot, 1)

    def hop_piece(p, target):
        def one_tile(t, carry):
            i = p * per_piece + t
            picked = []
            values = []
            for k in range(tile_k):
                at = (h * held + i) * tile_k + k
                picked.append(gathered[columns_ref[at]])
                sign = (1 - 2 * signs_ref[at]).astype(jnp.float32)
                values.append((weights[i, k].astype(jnp.float32) * sign).astype(jnp.bfloat16))
            left = jnp.concatenate(picked, axis=1)
            right = jnp.concatenate(values, axis=1)
            hopped = lax.dot_general(
                left, right, (((1,), (1,)), ((), ())), preferred_element_type=jnp.float32
            )
            target[t] = hopped.astype(jnp.bfloat16)
            return carry

        lax.fori_loop(0, per_piece, one_tile, 0)

    my_rows = pl.ds(pl.multiple_of(r * quarter, quarter), quarter)
    backs = []
    for k in (2, 1, 3):
        p = (r + k) % RING
        hop_piece(p, result.at[k - 1])
        copy = remote(
            result.at[k - 1], returned.at[:, my_rows], back_send.at[k - 1], back_recv.at[k - 1], ring_peer(p)
        )
        copy.start()
        backs.append(copy)
    hop_piece(r, returned.at[:, my_rows])
    for copy in backs:
        copy.wait()

    def hand_out(block, keep, give):
        copies = []
        for t in range(per_piece):
            columns = pl.ds(t * TILE, TILE)
            copy = remote(
                block.at[t, pl.ds(give, half)], other_ref.at[:, columns], last_send.at[t], last_recv.at[t], sibling
            )
            copy.start()
            copies.append(copy)
            copy = pltpu.make_async_copy(
                block.at[t, pl.ds(keep, half)], mine_ref.at[:, columns], load_sem.at[t]
            )
            copy.start()
            copies.append(copy)
        for copy in copies:
            copy.wait()

    @pl.when(core == 0)
    def _():
        hand_out(returned, 0, half)

    @pl.when(core == 1)
    def _():
        turn(returned, turned, side)
        hand_out(turned, half, 0)

    to_sibling.wait_send()
    for q in range(chunks):
        to_near[q].wait_send()
        forward(q).wait_send()

    @pl.when(core == 0)
    def _():
        for q in range(chunks):
            share_near(q).wait_send()

    @pl.when(core == 1)
    def _():
        for q in range(chunks):
            share_far(q).wait_send()


def hop_both(x, hop_tiles, columns, signs):
    half, side = x.shape
    tile_k = hop_tiles.shape[1]
    held = RING * (side // TILE)
    quarter = side // RING
    chunks = 4
    anywhere = pl.BlockSpec(memory_space=pl.ANY)
    scalars = pl.BlockSpec(memory_space=pltpu.SMEM)
    per_piece = side // TILE
    block = pltpu.VMEM((per_piece, side, TILE), jnp.bfloat16)
    dma = pltpu.SemaphoreType.DMA
    return pl.pallas_call(
        functools.partial(exchange_kernel, tile_k),
        in_specs=[scalars, scalars, anywhere, anywhere],
        out_specs=[anywhere, anywhere],
        out_shape=[jax.ShapeDtypeStruct(x.shape, jnp.bfloat16)] * 2,
        scratch_shapes=[
            block,
            block,
            block,
            block,
            block,
            pltpu.VMEM((2 * held, quarter, TILE), jnp.bfloat16),
            pltpu.VMEM((RING - 1, per_piece, quarter, TILE), jnp.bfloat16),
            block,
            pltpu.VMEM((held, tile_k, TILE, TILE), jnp.bfloat16),
            dma((per_piece,)),
            dma,
            dma,
            dma,
            dma((chunks,)),
            dma((chunks,)),
            dma((chunks,)),
            dma((chunks,)),
            dma((chunks,)),
            dma((chunks,)),
            dma((2, RING - 1)),
            dma((2, RING - 1)),
            dma((RING - 1,)),
            dma((RING - 1,)),
            dma((per_piece,)),
            dma((per_piece,)),
        ],
        compiler_params=pltpu.CompilerParams(
            collective_id=0, has_side_effects=True, vmem_limit_bytes=67043328
        ),
        cost_estimate=pl.CostEstimate(
            flops=2 * quarter * held * tile_k * TILE * TILE,
            bytes_accessed=8 * half * side + 2 * held * tile_k * TILE * TILE,
            transcendentals=0,
        ),
        name="hop_both",
    )(columns, signs, x, hop_tiles)


def sum_kernel(ups, downs, x_ref, out_ref, first, second, send_a, recv_a, send_b, recv_b):
    u = lax.axis_index("up")
    d = lax.axis_index("dn")
    barrier = pltpu.get_barrier_semaphore()
    for j in range(1, downs):
        pl.semaphore_signal(barrier, inc=1, device_id=(u, (d + j) % downs), device_id_type=MESH)
    for j in range(1, ups):
        pl.semaphore_signal(barrier, inc=1, device_id=((u + j) % ups, d), device_id_type=MESH)
    first[d] = x_ref[...]
    pl.semaphore_wait(barrier, ups + downs - 2)
    copies = []
    for j in range(1, downs):
        copy = pltpu.make_async_remote_copy(
            src_ref=x_ref, dst_ref=first.at[d], send_sem=send_a.at[j], recv_sem=recv_a.at[j],
            device_id=(u, (d + j) % downs), device_id_type=MESH,
        )
        copy.start()
        copies.append(copy)
    for copy in copies:
        copy.wait()
    total = first[0]
    for j in range(1, downs):
        total = total + first[j]
    second[u] = total
    copies = []
    for j in range(1, ups):
        copy = pltpu.make_async_remote_copy(
            src_ref=second.at[u], dst_ref=second.at[u], send_sem=send_b.at[j], recv_sem=recv_b.at[j],
            device_id=((u + j) % ups, d), device_id_type=MESH,
        )
        copy.start()
        copies.append(copy)
    for copy in copies:
        copy.wait()
    total = second[0]
    for j in range(1, ups):
        total = total + second[j]
    out_ref[...] = total


def sum_all(values):
    ups = lax.axis_size("up")
    downs = lax.axis_size("dn")
    tile = (8, TILE)
    packed = jnp.zeros(tile, jnp.float32)
    for row, value in enumerate(values):
        packed = packed.at[row].set(value)
    vmem = pl.BlockSpec(memory_space=pltpu.VMEM)
    summed = pl.pallas_call(
        functools.partial(sum_kernel, ups, downs),
        in_specs=[vmem],
        out_specs=vmem,
        out_shape=jax.ShapeDtypeStruct(tile, jnp.float32),
        scratch_shapes=[
            pltpu.VMEM((downs,) + tile, jnp.float32),
            pltpu.VMEM((ups,) + tile, jnp.float32),
            pltpu.SemaphoreType.DMA((downs,)),
            pltpu.SemaphoreType.DMA((downs,)),
            pltpu.SemaphoreType.DMA((ups,)),
            pltpu.SemaphoreType.DMA((ups,)),
        ],
        compiler_params=pltpu.CompilerParams(collective_id=1, has_side_effects=True),
        name="sum_all",
    )(packed)
    return [summed[row, 0] for row in range(len(values))]


def body(start_vector, hop_tiles, tile_columns, tile_signs, occupation):
    block_rows, block_cols = start_vector.shape
    columns = tile_columns.reshape(-1)
    signs = tile_signs.reshape(-1)
    row_start = lax.axis_index("up") * block_rows
    col_start = lax.axis_index("dn") * block_cols
    occ_rows = lax.dynamic_slice_in_dim(occupation, row_start, block_rows, 1).astype(jnp.bfloat16)
    occ_cols = lax.dynamic_slice_in_dim(occupation, col_start, block_cols, 1).astype(jnp.bfloat16)
    diagonal = (
        coupling * jnp.einsum("sa,sb->ab", occ_rows, occ_cols, preferred_element_type=jnp.float32)
    ).astype(jnp.bfloat16)
    start = start_vector.astype(jnp.float32)
    mine, other = hop_both(start_vector, hop_tiles, columns, signs)
    work = mine.astype(jnp.float32) + other.astype(jnp.float32) + diagonal * start
    total, cross, square = sum_all(
        [jnp.sum(start * start), jnp.sum(work * start), jnp.sum(work * work)]
    )
    scale = 1.0 / jnp.maximum(jnp.sqrt(total), 1.0)
    length = total / jnp.maximum(total, 1.0)
    alpha = cross * scale * scale
    residual = square * scale * scale - 2.0 * alpha * alpha + alpha * alpha * length
    beta = jnp.sqrt(jnp.maximum(residual, 1.0))
    alphas, betas = [alpha], [beta]
    length = residual / jnp.maximum(residual, 1.0)
    previous = start * scale
    vector = (work * scale - alpha * previous) / beta
    for _ in range(STEPS - 1):
        mine, other = hop_both(vector.astype(jnp.bfloat16), hop_tiles, columns, signs)
        work = mine.astype(jnp.float32) + other.astype(jnp.float32) + diagonal * vector - beta * previous
        alpha, square = sum_all([jnp.sum(work * vector), jnp.sum(work * work)])
        residual = square - 2.0 * alpha * alpha + alpha * alpha * length
        beta = jnp.sqrt(jnp.maximum(residual, 1.0))
        alphas.append(alpha)
        betas.append(beta)
        length = residual / jnp.maximum(residual, 1.0)
        previous, vector = vector, (work - alpha * vector) / beta
    return (vector.astype(jnp.bfloat16), jnp.stack(alphas), jnp.stack(betas))


def solution(mesh):
    placed = (P("up", "dn"), P(), P(), P(), P())
    return jax.shard_map(
        body, mesh=mesh, in_specs=placed, out_specs=(P("up", "dn"), P(), P()), check_vma=False
    )
```

time: 633 us -> 402 us (0.64)
  blocking collectives: 298 us -> 0 us
  Pallas kernels: 97.9 us -> 350 us
  local copies, waits for them, and re-layouts: 78.1 us -> 10.4 us
  waiting for transfers between devices: 53.3 us -> 0 us
  starting transfers between devices: 35 us -> 0 us
  other arithmetic: 50.9 us -> 24.4 us
    pallas_call x4, Pallas kernels: 97.9 us -> 350 us  [the longest x2 325 us: hop_both(): pl.pallas_call(functools.partial(exchange_kernel, tile_k), in_specs=[scal...]
    psum x3 -> x0, blocking collectives: 215 us -> none  [the longest x2 129 us: body(): lax.psum((jnp.sum(work * vector), jnp.sum(work * work)), ('up', 'dn'))]
    all_to_all x2 -> x0, blocking collectives: 83.6 us -> none  [body(): up = lax.all_to_all(up, 'up', 0, 0, tiled=True)]
    all_to_all x6 -> x0, waiting for transfers between devices: 53.3 us -> none  [the longest x2 30.2 us: body(): up = lax.all_to_all(up, 'up', 0, 0, tiled=True)]
    all_to_all x6 -> x0, starting transfers between devices: 35 us -> none  [the longest x4 25.5 us: body(): down = lax.all_to_all(down, 'dn', 0, 0, tiled=True)]
    transpose x4 -> x0, local copies, waits for them, and re-layouts: 32 us -> none  [the longest x1 22.8 us: body(): stacked = signed.transpose(0, 1, 3, 2).reshape(tiles, tile_k * tile, tile)]
    reshape x6 -> x1, local copies, waits for them, and re-layouts: 25.6 us -> 0.77 us  [body(): signs = tile_signs.reshape(-1)]
    convert_element_type x3 -> x0, local copies, waits for them, and re-layouts: 14.3 us -> none  [the longest x2 14.2 us: body(): hopped = hopped_up.astype(jnp.float32) + hopped_down.astype(jnp.float32)]
  transfers between devices with their start and end apart: 6 -> 0, of which waited for: 3 -> 0; matrix products, arithmetic and copies ran while one was open for 15% -> 0% of each run, Pallas kernels for 16% -> 0%
where the time goes in v1:
time: 402 us; the launch traced here: 401 us
  Pallas kernels  350 us (87%)
  other arithmetic  24.4 us (6%)
  local copies, waits for them, and re-layouts  10.4 us (3%)
  matrix products  8.89 us (2%)
  between operations  7.12 us (2%)
    pallas_call x2, Pallas kernels, hop_both(): pl.pallas_call(functools.partial(exchange_kernel, tile_k), in_specs=[scal...  325 us
    pallas_call x2, Pallas kernels, sum_all(): pl.pallas_call(functools.partial(sum_kernel, ups, downs), in_specs=[vmem]...  25.3 us
    reduce_sum x1, other arithmetic, body(): alpha, square = sum_all([jnp.sum(work * vector), jnp.sum(work * work)])  9.6 us
    dot_general x1, matrix products, body(): jnp.einsum('sa,sb->ab', occ_rows, occ_cols, preferred_element_type=jnp.fl...  8.89 us

profile of v1, /device:TPU:1, one launch (start us, length us, event | category | flops | bytes accessed | tf_op | source)
XLA Modules:
  0.0 401.3 jit_solution(9750928556867263559)
XLA Ops:
  0.6 0.8 copy.8
  1.4 0.8 reshape.117.columns_ref
  2.2 0.8 copy.9
  3.0 0.8 reshape.118.signs_ref
  3.7 165.2 %hop_both.2 = (bf16[832,1664]{1,0:T(8,128)(2,1)}, bf16[832,1664]{1,0:T(8,128)(2,1)}) custom-call(s32[520]{0:T(1024)} %reshape.117.columns_ref, s32[520]{0:T(1024)} %reshape.118.signs_ref, bf16[832,1664]{1,0:T(8,128)(2,1)} %x_ref.1, bf16[104,5,128,128]{3,2,1,0:T(8,128)(2,1)} %tiles_ref.3), custom_call_target="tpu_custom_call" | custom-call | flops 3544186880 | bytes 19595264 | tf_op jit(solution)/shard_map/hop_both/pallas_call | solution.py:294
  168.9 0.0 copy-start
  168.9 8.9 %multiply_reduce_fusion.2 = (f32[]{:T(128)}, f32[]{:T(128)}, f32[]{:T(128)}, bf16[832,1664]{1,0:T(8,128)(2,1)}) fusion(bf16[832,1664]{1,0:T(8,128)(2,1)} %x_ref.1, bf16[832,1664]{1,0:T(8,128)(2,1)} %get-tuple-element.68, bf16[832,1664]{1,0:T(8,128)(2,1)} %get-tuple-element.67, s32[16,13312]{1,0:T(8,128)} %param.19, s32[]{:T(128)S(6)} %select_n.7, ...), kind=kOutput, calls=%fused_computation.17 | convolution fusion | flops 65108992 | bytes 11239444 | tf_op jit(solution)/shard_map/sa,sb->ab/dot_general | solution.py:414
  177.8 0.6 broadcast.108
  178.5 0.6 broadcast.107
  179.2 0.7 scatter.24
  179.9 0.1 scatter.30
  180.0 0.0 copy-start.2
  180.0 0.6 copy-done.2
  180.6 12.3 %sum_all.2 = f32[8,128]{1,0:T(8,128)} custom-call(f32[8,128]{1,0:T(8,128)} %copy-done.2), custom_call_target="tpu_custom_call" | custom-call | tf_op jit(solution)/shard_map/sum_all/pallas_call | solution.py:386
  192.9 1.3 fusion.14
  197.4 0.0 copy-done
  197.4 6.6 %fusion.11 = (bf16[832,1664]{1,0:T(8,128)(2,1)}, f32[832,1664]{1,0:T(8,128)}) fusion(f32[]{:T(128)} %sqrt.10, f32[]{:T(128)} %mul.106, f32[]{:T(128)S(6)} %div.21, bf16[832,1664]{1,0:T(8,128)(2,1)S(1)} %copy-done, bf16[832,1664]{1,0:T(8,128)(2,1)} %get-tuple-element.84, bf16[832,1664]{1,0:T(8,128)(2,1)} %get-tuple-element.68, ...), kind=kLoop, calls=%fused_computation.24 | loop fusion | flops 17997824 | bytes 19382284 | tf_op jit(solution)/shard_map/convert_element_type | solution.py:432
  204.0 160.0 %hop_both.3 = (bf16[832,1664]{1,0:T(8,128)(2,1)}, bf16[832,1664]{1,0:T(8,128)(2,1)}) custom-call(s32[520]{0:T(1024)} %reshape.117.columns_ref, s32[520]{0:T(1024)} %reshape.118.signs_ref, bf16[832,1664]{1,0:T(8,128)(2,1)} %get-tuple-element.77.x_ref, bf16[104,5,128,128]{3,2,1,0:T(8,128)(2,1)} %tiles_ref.3), custom_call_target="tpu_custom_call" | custom-call | flops 3544186880 | bytes 19595264 | tf_op jit(solution)/shard_map/hop_both/pallas_call | solution.py:294
  363.9 9.6 %multiply_reduce_fusion = (f32[]{:T(128)}, f32[]{:T(128)}, f32[832,1664]{1,0:T(8,128)}) fusion(f32[832,1664]{1,0:T(8,128)} %get-tuple-element.78, f32[]{:T(128)S(6)} %div.21, bf16[832,1664]{1,0:T(8,128)(2,1)} %x_ref.1, f32[]{:T(128)} %sqrt.10, bf16[832,1664]{1,0:T(8,128)(2,1)} %get-tuple-element.84, bf16[832,1664]{1,0:T(8,128)(2,1)} %get-tuple-element.70, ...), kind=kLoop, calls=%fused_computation.15 | loop fusion | flops 19382272 | bytes 22151184 | tf_op jit(solution)/shard_map/reduce_sum | solution.py:434
  373.5 0.6 broadcast.109
  374.2 0.7 scatter.33
  374.8 0.1 scatter.34
  374.9 0.0 copy-start.1
  374.9 0.6 copy-done.1
  375.5 13.0 %sum_all.3 = f32[8,128]{1,0:T(8,128)} custom-call(f32[8,128]{1,0:T(8,128)} %copy-done.1), custom_call_target="tpu_custom_call" | custom-call | tf_op jit(solution)/shard_map/sum_all/pallas_call | solution.py:386
  388.5 1.3 fusion.13
  393.0 7.1 %divide_convert_fusion = bf16[832,1664]{1,0:T(8,128)(2,1)} fusion(f32[832,1664]{1,0:T(8,128)} %get-tuple-element.76, f32[832,1664]{1,0:T(8,128)} %get-tuple-element.78, f32[]{:T(128)} %sqrt.11, f32[]{:T(128)} %bitcast.5), kind=kLoop, calls=%fused_computation.14 | loop fusion | flops 5537792 | bytes 13844488 | tf_op jit(solution)/shard_map/convert_element_type | solution.py:441
  400.1 1.2 pad_maximum_fusion
  (3 shorter events, 0.1 us)
Async XLA Ops:
  168.9 28.4 %copy-start = (bf16[832,1664]{1,0:T(8,128)(2,1)S(1)}, bf16[832,1664]{1,0:T(8,128)(2,1)}, u32[]{:S(2)}) copy-start(bf16[832,1664]{1,0:T(8,128)(2,1)} %x_ref.1) | copy-start | bytes 8306692
  180.0 0.6 copy-start.2
  374.9 0.6 copy-start.1

commit v2 on v1

--- a/solution.py
+++ b/solution.py
@@ -25,16 +25,16 @@
     return (y_lo * 8 + x * 2 + core, y_hi * 4 + z)
 
 
-def turn(source, target, side):
-    tiles = side // TILE
-
-    def one_row(i, carry):
-        at = pl.multiple_of(i * TILE, TILE)
-        for j in range(tiles):
-            target[i, j * TILE : (j + 1) * TILE, :] = source[j, pl.ds(at, TILE), :].T
-        return carry
-
-    lax.fori_loop(0, tiles, one_row, 0)
+def turn_tile(source, target, i, tiles):
+    for j in range(tiles):
+        target[i, j * TILE : (j + 1) * TILE, :] = source[j, i * TILE : (i + 1) * TILE, :].T
+
+
+PARTS = 2
+CUTS = (112, 96)
+CHUNKS = 8
+GROUPS = {1: ((0, 1), (7, 1)), 3: ((1, 2), (8, 1)), 5: ((3, 1), (9, 2)), 7: ((4, 3), (11, 2))}
+GROUP_AT = {0: 0, 7: 1, 1: 2, 8: 3, 3: 4, 9: 5, 4: 6, 11: 7}
 
 
 def exchange_kernel(
@@ -50,7 +50,8 @@
     far,
     turned,
     turned_near,
-    gathered,
+    gathered_a,
+    gathered_b,
     result,
     returned,
     weights,
@@ -66,6 +67,8 @@
     share_recv,
     ring_send,
     ring_recv,
+    late_send,
+    late_recv,
     back_send,
     back_recv,
     last_send,
@@ -74,10 +77,10 @@
     half = x_ref.shape[0]
     side = 2 * half
     quarter = side // RING
-    chunks = near_send.shape[0]
-    step = half // chunks
+    piece = quarter // PARTS
     per_piece = side // TILE
     held = RING * per_piece
+    gathered = (gathered_a, gathered_b)
     y_lo, x, core, y_hi, z = place()
     r = z + core * (x - z)
     h = y_hi + core * (y_lo - y_hi)
@@ -93,11 +96,17 @@
             src_ref=src, dst_ref=dst, send_sem=send, recv_sem=recv, device_id=to, device_id_type=MESH
         )
 
+    def rows_of(p, part):
+        start = (p // 2) * half + (p % 2) * piece + part * quarter
+        return pl.ds(pl.multiple_of(start, 16), piece)
+
+    starts = [(q // 2) * piece + (q % 2) * CUTS[0] for q in range(CHUNKS)]
+    sizes = [CUTS[q % 2] for q in range(CHUNKS)]
+
     barrier = pltpu.get_barrier_semaphore()
     greeted = [sibling, near_chip, far_chip] + [ring_peer((r + k) % RING) for k in range(1, RING)]
     for to in greeted:
         pl.semaphore_signal(barrier, inc=1, device_id=to, device_id_type=MESH)
-    pl.semaphore_wait(barrier, len(greeted))
 
     base = pl.multiple_of(core * half, half)
     my_half = pl.ds(base, half)
@@ -108,110 +117,190 @@
         )
         copy.start()
         loads.append(copy)
-    for copy in loads:
-        copy.wait()
+    with jax.named_scope("barrier"):
+        pl.semaphore_wait(barrier, len(greeted))
+    with jax.named_scope("load"):
+        for copy in loads:
+            copy.wait()
     to_sibling = remote(own.at[:, my_half], own.at[:, my_half], sib_send, sib_recv, sibling)
     to_sibling.start()
-    to_near = []
-    for q in range(chunks):
-        rows = pl.ds(pl.multiple_of(base + q * step, step), step)
-        copy = remote(
-            own.at[:, rows], near.at[:, rows], near_send.at[q], near_recv.at[q], near_chip
-        )
-        copy.start()
-        to_near.append(copy)
+
+    def to_near(q):
+        rows = pl.ds(pl.multiple_of(base + starts[q], 16), sizes[q])
+        return remote(own.at[:, rows], near.at[:, rows], near_send.at[q], near_recv.at[q], near_chip)
+
+    for q in range(CHUNKS):
+        to_near(q).start()
     first = pl.multiple_of(h * held, held)
     load_tiles = pltpu.make_async_copy(tiles_ref.at[pl.ds(first, held)], weights, tiles_sem)
     load_tiles.start()
-    to_sibling.wait_recv()
-
-    def ring_out(block, slot, which):
-        copies = []
-        for k in (2, 1, 3):
-            p = (r + k) % RING
-            rows = pl.ds(pl.multiple_of(p * quarter, quarter), quarter)
-            copy = remote(
-                block.at[:, rows], gathered.at[slot], ring_send.at[which, k - 1], ring_recv.at[which, k - 1], ring_peer(p)
-            )
+    with jax.named_scope("sibling"):
+        to_sibling.wait_recv()
+
+    own_slot = pl.ds((h * RING + r) * per_piece, per_piece)
+    near_start = ((1 - h) * RING + r) * per_piece
+    near_slot = pl.ds(near_start, per_piece)
+
+    def own_copy(block, part, k):
+        p = (r + k) % RING
+        return remote(
+            block.at[:, rows_of(p, part)],
+            gathered[part].at[own_slot],
+            ring_send.at[part, k - 1],
+            ring_recv.at[part, k - 1],
+            ring_peer(p),
+        )
+
+    def own_out(block):
+        for part in range(PARTS):
+            for k in (2, 1, 3):
+                own_copy(block, part, k).start()
+        for part in range(PARTS):
+            gathered[part][own_slot] = block[:, rows_of(r, part)]
+
+    @pl.when(core == 0)
+    def _():
+        own_out(own)
+
+    @pl.when(core == 1)
+    def _():
+        with jax.named_scope("turn_own"):
+            for i in range(per_piece):
+                turn_tile(own, turned, i, per_piece)
+        own_out(turned)
+
+    def half_rows(of, q):
+        return pl.ds(of * half + starts[q], sizes[q])
+
+    def forward(q):
+        rows = pl.ds(pl.multiple_of(base + starts[q], 16), sizes[q])
+        return remote(near.at[:, rows], far.at[:, rows], far_send.at[q], far_recv.at[q], far_chip)
+
+    def share_near(q):
+        rows = half_rows(0, q)
+        return remote(near.at[:, rows], near.at[:, rows], share_send.at[q], share_recv.at[q], sibling)
+
+    def share_far(q):
+        rows = half_rows(1, q)
+        return remote(far.at[:, rows], far.at[:, rows], share_send.at[q], share_recv.at[q], sibling)
+
+    def late_down(of, q):
+        p = 2 * of + (q // 2) % 2
+        part, sub = q // 4, q % 2
+        k = (p - r) % RING
+        at = (part * 2 + sub) * RING + k
+        rows = pl.ds(sub * CUTS[0], sizes[q])
+        return p, remote(
+            far.at[:, half_rows(of, q)],
+            gathered[part].at[near_slot, rows],
+            late_send.at[at],
+            late_recv.at[at],
+            ring_peer(p),
+        )
+
+    def pass_down(of, q):
+        p, copy = late_down(of, q)
+
+        @pl.when(p != r)
+        def _():
             copy.start()
-            copies.append(copy)
-        rows = pl.ds(pl.multiple_of(r * quarter, quarter), quarter)
-        gathered[slot] = block[:, rows]
-        return copies
-
-    own_slot = pl.ds((h * RING + r) * per_piece, per_piece)
-    near_slot = pl.ds(((1 - h) * RING + r) * per_piece, per_piece)
-
-    def ring_copies(block, slot, which):
+
+        @pl.when(p == r)
+        def _():
+            part, sub = q // 4, q % 2
+            gathered[part][near_slot, sub * CUTS[0] : sub * CUTS[0] + sizes[q]] = far[:, half_rows(of, q)]
+
+    def late_up(start, count, part, k):
+        p = (r + k) % RING
+        at = (GROUP_AT[start] * PARTS + part) * RING + k
+        tiles = pl.ds(start, count)
+        return remote(
+            turned_near.at[tiles, rows_of(p, part)],
+            gathered[part].at[pl.ds(near_start + start, count)],
+            late_send.at[at],
+            late_recv.at[at],
+            ring_peer(p),
+        )
+
+    def pass_up(start, count):
+        for i in range(start, start + count):
+            turn_tile(near, turned_near, i, per_piece)
+        for part in range(PARTS):
+            for k in (2, 1, 3):
+                late_up(start, count, part, k).start()
+        tiles = pl.ds(start, count)
+        for part in range(PARTS):
+            gathered[part][pl.ds(near_start + start, count)] = turned_near[tiles, rows_of(r, part)]
+
+    @pl.when(core == 0)
+    def _():
+        for q in range(CHUNKS + 1):
+            if q < CHUNKS:
+                with jax.named_scope(f"near{q}"):
+                    to_near(q).wait_recv()
+                forward(q).start()
+                share_near(q).start()
+            if q >= 1:
+                with jax.named_scope(f"far{q - 1}"):
+                    forward(q - 1).wait_recv()
+                pass_down(0, q - 1)
+                with jax.named_scope(f"share{q - 1}"):
+                    share_far(q - 1).wait_recv()
+                pass_down(1, q - 1)
+
+    @pl.when(core == 1)
+    def _():
+        for q in range(CHUNKS + 1):
+            if q < CHUNKS:
+                with jax.named_scope(f"near{q}"):
+                    to_near(q).wait_recv()
+                forward(q).start()
+            if q >= 1:
+                with jax.named_scope(f"far{q - 1}"):
+                    forward(q - 1).wait_recv()
+                share_far(q - 1).start()
+            if q < CHUNKS:
+                with jax.named_scope(f"share{q}"):
+                    share_near(q).wait_recv()
+                for start, count in GROUPS.get(q, ()):
+                    pass_up(start, count)
+
+    with jax.named_scope("tiles"):
+        load_tiles.wait()
+
+    def arrivals(part):
         for k in range(1, RING):
-            p = (r + k) % RING
-            rows = pl.ds(pl.multiple_of(p * quarter, quarter), quarter)
-            remote(
-                block.at[:, rows], gathered.at[slot], ring_send.at[which, k - 1], ring_recv.at[which, k - 1], ring_peer(p)
-            ).wait()
-
-    @pl.when(core == 0)
-    def _():
-        ring_out(own, own_slot, 0)
-
-    @pl.when(core == 1)
-    def _():
-        turn(own, turned, side)
-        ring_out(turned, own_slot, 0)
-
-    def chunk_rows(of, q):
-        return pl.ds(of * half + q * step, step)
-
-    def forward(q):
-        rows = pl.ds(pl.multiple_of(base + q * step, step), step)
-        return remote(near.at[:, rows], far.at[:, rows], far_send.at[q], far_recv.at[q], far_chip)
-
-    def share_near(q):
-        rows = chunk_rows(0, q)
-        return remote(near.at[:, rows], near.at[:, rows], share_send.at[q], share_recv.at[q], sibling)
-
-    def share_far(q):
-        rows = chunk_rows(1, q)
-        return remote(far.at[:, rows], far.at[:, rows], share_send.at[q], share_recv.at[q], sibling)
-
-    for q in range(chunks):
-        to_near[q].wait_recv()
-        forward(q).start()
+            own_copy(own, part, k).wait_recv()
 
         @pl.when(core == 0)
         def _():
-            share_near(q).start()
-
-    @pl.when(core == 0)
-    def _():
-        for q in range(chunks):
-            forward(q).wait_recv()
-        for q in range(chunks):
-            share_far(q).wait_recv()
-        ring_out(far, near_slot, 1)
-
-    @pl.when(core == 1)
-    def _():
-        for q in range(chunks):
-            share_near(q).wait_recv()
-        turn(near, turned_near, side)
-        ring_out(turned_near, near_slot, 1)
-        for q in range(chunks):
-            forward(q).wait_recv()
-            share_far(q).start()
-
-    load_tiles.wait()
-    ring_copies(own, own_slot, 0)
-    ring_copies(far, near_slot, 1)
-
-    def hop_piece(p, target):
+            for sub in range(2):
+                for k in range(1, RING):
+                    at = (part * 2 + sub) * RING + k
+                    rows = pl.ds(sub * CUTS[0], CUTS[sub])
+                    remote(
+                        far.at[:, rows],
+                        gathered[part].at[near_slot, rows],
+                        late_send.at[at],
+                        late_recv.at[at],
+                        ring_peer((r + k) % RING),
+                    ).wait_recv()
+
+        @pl.when(core == 1)
+        def _():
+            for groups in GROUPS.values():
+                for start, count in groups:
+                    for k in range(1, RING):
+                        late_up(start, count, part, k).wait_recv()
+
+    def hop_piece(part, p, target):
         def one_tile(t, carry):
             i = p * per_piece + t
             picked = []
             values = []
             for k in range(tile_k):
                 at = (h * held + i) * tile_k + k
-                picked.append(gathered[columns_ref[at]])
+                picked.append(gathered[part][columns_ref[at]])
                 sign = (1 - 2 * signs_ref[at]).astype(jnp.float32)
                 values.append((weights[i, k].astype(jnp.float32) * sign).astype(jnp.bfloat16))
             left = jnp.concatenate(picked, axis=1)
@@ -224,19 +313,27 @@
 
         lax.fori_loop(0, per_piece, one_tile, 0)
 
-    my_rows = pl.ds(pl.multiple_of(r * quarter, quarter), quarter)
-    backs = []
-    for k in (2, 1, 3):
-        p = (r + k) % RING
-        hop_piece(p, result.at[k - 1])
-        copy = remote(
-            result.at[k - 1], returned.at[:, my_rows], back_send.at[k - 1], back_recv.at[k - 1], ring_peer(p)
-        )
-        copy.start()
-        backs.append(copy)
-    hop_piece(r, returned.at[:, my_rows])
-    for copy in backs:
-        copy.wait()
+    def back_copy(part, k):
+        return remote(
+            result.at[part, k - 1],
+            returned.at[:, rows_of(r, part)],
+            back_send.at[part, k - 1],
+            back_recv.at[part, k - 1],
+            ring_peer((r + k) % RING),
+        )
+
+    for part in range(PARTS):
+        with jax.named_scope(f"arrive{part}"):
+            arrivals(part)
+        with jax.named_scope(f"hop{part}"):
+            for k in (2, 1, 3):
+                hop_piece(part, (r + k) % RING, result.at[part, k - 1])
+                back_copy(part, k).start()
+            hop_piece(part, r, returned.at[:, rows_of(r, part)])
+    with jax.named_scope("back"):
+        for part in range(PARTS):
+            for k in range(1, RING):
+                back_copy(part, k).wait()
 
     def hand_out(block, keep, give):
         copies = []
@@ -255,29 +352,48 @@
         for copy in copies:
             copy.wait()
 
+    for part in range(PARTS):
+        for k in range(1, RING):
+            own_copy(own, part, k).wait_send()
+
     @pl.when(core == 0)
     def _():
-        hand_out(returned, 0, half)
+        with jax.named_scope("out0"):
+            hand_out(returned, 0, half)
 
     @pl.when(core == 1)
     def _():
-        turn(returned, turned, side)
-        hand_out(turned, half, 0)
+        with jax.named_scope("turn_back"):
+            for i in range(per_piece):
+                turn_tile(returned, turned, i, per_piece)
+        with jax.named_scope("out1"):
+            hand_out(turned, half, 0)
 
     to_sibling.wait_send()
-    for q in range(chunks):
-        to_near[q].wait_send()
+    for q in range(CHUNKS):
+        to_near(q).wait_send()
         forward(q).wait_send()
 
     @pl.when(core == 0)
     def _():
-        for q in range(chunks):
+        for q in range(CHUNKS):
             share_near(q).wait_send()
+            for of in range(2):
+                p, copy = late_down(of, q)
+
+                @pl.when(p != r)
+                def _():
+                    copy.wait_send()
 
     @pl.when(core == 1)
     def _():
-        for q in range(chunks):
+        for q in range(CHUNKS):
             share_far(q).wait_send()
+        for groups in GROUPS.values():
+            for start, count in groups:
+                for part in range(PARTS):
+                    for k in range(1, RING):
+                        late_up(start, count, part, k).wait_send()
 
 
 def hop_both(x, hop_tiles, columns, signs):
@@ -285,7 +401,7 @@
     tile_k = hop_tiles.shape[1]
     held = RING * (side // TILE)
     quarter = side // RING
-    chunks = 4
+    piece = quarter // PARTS
     anywhere = pl.BlockSpec(memory_space=pl.ANY)
     scalars = pl.BlockSpec(memory_space=pltpu.SMEM)
     per_piece = side // TILE
@@ -302,24 +418,27 @@
             block,
             block,
             block,
-            pltpu.VMEM((2 * held, quarter, TILE), jnp.bfloat16),
-            pltpu.VMEM((RING - 1, per_piece, quarter, TILE), jnp.bfloat16),
+            pltpu.VMEM((2 * held, piece, TILE), jnp.bfloat16),
+            pltpu.VMEM((2 * held, piece, TILE), jnp.bfloat16),
+            pltpu.VMEM((PARTS, RING - 1, per_piece, piece, TILE), jnp.bfloat16),
             block,
             pltpu.VMEM((held, tile_k, TILE, TILE), jnp.bfloat16),
             dma((per_piece,)),
             dma,
             dma,
             dma,
-            dma((chunks,)),
-            dma((chunks,)),
-            dma((chunks,)),
-            dma((chunks,)),
-            dma((chunks,)),
-            dma((chunks,)),
-            dma((2, RING - 1)),
-            dma((2, RING - 1)),
-            dma((RING - 1,)),
-            dma((RING - 1,)),
+            dma((CHUNKS,)),
+            dma((CHUNKS,)),
+            dma((CHUNKS,)),
+            dma((CHUNKS,)),
+            dma((CHUNKS,)),
+            dma((CHUNKS,)),
+            dma((PARTS, RING - 1)),
+            dma((PARTS, RING - 1)),
+            dma((len(GROUP_AT) * PARTS * RING,)),
+            dma((len(GROUP_AT) * PARTS * RING,)),
+            dma((PARTS, RING - 1)),
+            dma((PARTS, RING - 1)),
             dma((per_piece,)),
             dma((per_piece,)),
         ],

time: 402 us -> 328 us (0.82)
  Pallas kernels: 350 us -> 277 us
    pallas_call x2, Pallas kernels: 325 us -> 248 us  [hop_both(): pl.pallas_call(functools.partial(exchange_kernel, tile_k), in_specs=[scal...]
where the time goes in v2:
time: 328 us
  Pallas kernels  277 us (84%)
  other arithmetic  24.4 us (7%)
  local copies, waits for them, and re-layouts  10.4 us (3%)
  matrix products  8.89 us (3%)
  between operations  7.12 us (2%)
    pallas_call x2, Pallas kernels, hop_both(): pl.pallas_call(functools.partial(exchange_kernel, tile_k), in_specs=[scal...  248 us
    pallas_call x2, Pallas kernels, sum_all(): pl.pallas_call(functools.partial(sum_kernel, ups, downs), in_specs=[vmem]...  28.9 us
    reduce_sum x1, other arithmetic, body(): alpha, square = sum_all([jnp.sum(work * vector), jnp.sum(work * work)])  9.6 us
    dot_general x1, matrix products, body(): jnp.einsum('sa,sb->ab', occ_rows, occ_cols, preferred_element_type=jnp.fl...  8.89 us
    convert_element_type x1, other arithmetic, body(): return (vector.astype(jnp.bfloat16), jnp.stack(alphas), jnp.stack(betas))  7.06 us
    convert_element_type x1, other arithmetic, body(): vector.astype(jnp.bfloat16)  6.57 us

profile of v2, /device:TPU:1, one launch (start us, length us, event | category | flops | bytes accessed | tf_op | source)
XLA Modules:
  0.0 327.7 jit_solution(16561052644842984913)
XLA Ops:
  0.6 0.8 copy.8
  1.4 0.8 reshape.117.columns_ref
  2.2 0.8 copy.9
  3.0 0.8 reshape.118.signs_ref
  3.7 126.0 %hop_both.2 = (bf16[832,1664]{1,0:T(8,128)(2,1)}, bf16[832,1664]{1,0:T(8,128)(2,1)}) custom-call(s32[520]{0:T(1024)} %reshape.117.columns_ref, s32[520]{0:T(1024)} %reshape.118.signs_ref, bf16[832,1664]{1,0:T(8,128)(2,1)} %x_ref.1, bf16[104,5,128,128]{3,2,1,0:T(8,128)(2,1)} %tiles_ref.3), custom_call_target="tpu_custom_call" | custom-call | flops 3544186880 | bytes 19595264 | tf_op jit(solution)/shard_map/hop_both/pallas_call | solution.py:410
  129.8 0.0 copy-start
  129.8 8.9 %multiply_reduce_fusion.2 = (f32[]{:T(128)}, f32[]{:T(128)}, f32[]{:T(128)}, bf16[832,1664]{1,0:T(8,128)(2,1)}) fusion(bf16[832,1664]{1,0:T(8,128)(2,1)} %x_ref.1, bf16[832,1664]{1,0:T(8,128)(2,1)} %get-tuple-element.68, bf16[832,1664]{1,0:T(8,128)(2,1)} %get-tuple-element.67, s32[16,13312]{1,0:T(8,128)} %param.19, s32[]{:T(128)S(6)} %select_n.7, ...), kind=kOutput, calls=%fused_computation.17 | convolution fusion | flops 65108992 | bytes 11239444 | tf_op jit(solution)/shard_map/sa,sb->ab/dot_general | solution.py:533
  138.7 0.6 broadcast.108
  139.3 0.6 broadcast.107
  140.0 0.7 scatter.24
  140.7 0.1 scatter.30
  140.8 0.0 copy-start.2
  140.8 0.6 copy-done.2
  141.4 14.8 %sum_all.2 = f32[8,128]{1,0:T(8,128)} custom-call(f32[8,128]{1,0:T(8,128)} %copy-done.2), custom_call_target="tpu_custom_call" | custom-call | tf_op jit(solution)/shard_map/sum_all/pallas_call | solution.py:505
  156.2 1.3 fusion.14
  160.7 0.0 copy-done
  160.7 6.6 %fusion.11 = (bf16[832,1664]{1,0:T(8,128)(2,1)}, f32[832,1664]{1,0:T(8,128)}) fusion(f32[]{:T(128)} %sqrt.10, f32[]{:T(128)} %mul.106, f32[]{:T(128)S(6)} %div.21, bf16[832,1664]{1,0:T(8,128)(2,1)S(1)} %copy-done, bf16[832,1664]{1,0:T(8,128)(2,1)} %get-tuple-element.84, bf16[832,1664]{1,0:T(8,128)(2,1)} %get-tuple-element.68, ...), kind=kLoop, calls=%fused_computation.24 | loop fusion | flops 17997824 | bytes 19382284 | tf_op jit(solution)/shard_map/convert_element_type | solution.py:551
  167.2 121.9 %hop_both.3 = (bf16[832,1664]{1,0:T(8,128)(2,1)}, bf16[832,1664]{1,0:T(8,128)(2,1)}) custom-call(s32[520]{0:T(1024)} %reshape.117.columns_ref, s32[520]{0:T(1024)} %reshape.118.signs_ref, bf16[832,1664]{1,0:T(8,128)(2,1)} %get-tuple-element.77.x_ref, bf16[104,5,128,128]{3,2,1,0:T(8,128)(2,1)} %tiles_ref.3), custom_call_target="tpu_custom_call" | custom-call | flops 3544186880 | bytes 19595264 | tf_op jit(solution)/shard_map/hop_both/pallas_call | solution.py:410
  289.1 9.6 %multiply_reduce_fusion = (f32[]{:T(128)}, f32[]{:T(128)}, f32[832,1664]{1,0:T(8,128)}) fusion(f32[832,1664]{1,0:T(8,128)} %get-tuple-element.78, f32[]{:T(128)S(6)} %div.21, bf16[832,1664]{1,0:T(8,128)(2,1)} %x_ref.1, f32[]{:T(128)} %sqrt.10, bf16[832,1664]{1,0:T(8,128)(2,1)} %get-tuple-element.84, bf16[832,1664]{1,0:T(8,128)(2,1)} %get-tuple-element.70, ...), kind=kLoop, calls=%fused_computation.15 | loop fusion | flops 19382272 | bytes 22151184 | tf_op jit(solution)/shard_map/reduce_sum | solution.py:553
  298.7 0.6 broadcast.109
  299.4 0.7 scatter.33
  300.0 0.1 scatter.34
  300.1 0.0 copy-start.1
  300.1 0.6 copy-done.1
  300.7 14.1 %sum_all.3 = f32[8,128]{1,0:T(8,128)} custom-call(f32[8,128]{1,0:T(8,128)} %copy-done.1), custom_call_target="tpu_custom_call" | custom-call | tf_op jit(solution)/shard_map/sum_all/pallas_call | solution.py:505
  314.9 1.3 fusion.13
  319.4 7.1 %divide_convert_fusion = bf16[832,1664]{1,0:T(8,128)(2,1)} fusion(f32[832,1664]{1,0:T(8,128)} %get-tuple-element.76, f32[832,1664]{1,0:T(8,128)} %get-tuple-element.78, f32[]{:T(128)} %sqrt.11, f32[]{:T(128)} %bitcast.5), kind=kLoop, calls=%fused_computation.14 | loop fusion | flops 5537792 | bytes 13844488 | tf_op jit(solution)/shard_map/convert_element_type | solution.py:560
  326.4 1.2 pad_maximum_fusion
  (3 shorter events, 0.1 us)
Async XLA Ops:
  129.8 30.9 %copy-start = (bf16[832,1664]{1,0:T(8,128)(2,1)S(1)}, bf16[832,1664]{1,0:T(8,128)(2,1)}, u32[]{:S(2)}) copy-start(bf16[832,1664]{1,0:T(8,128)(2,1)} %x_ref.1) | copy-start | bytes 8306692
  140.8 0.6 copy-start.2
  300.1 0.6 copy-start.1

commit v3 on v2

v3 whole, which is shorter than its diff:
```python
import functools

import jax
import jax.numpy as jnp
from jax import lax
from jax.experimental import pallas as pl
from jax.experimental.pallas import tpu as pltpu
from jax.sharding import PartitionSpec as P

STEPS = 2
RING = 4
TILE = 128
MESH = pl.DeviceIdType.MESH

coupling = 4.0


def place():
    u = lax.axis_index("up")
    d = lax.axis_index("dn")
    return u // 8, (u // 2) % 4, u % 2, d // 4, d % 4


def device(y_lo, x, core, y_hi, z):
    return (y_lo * 8 + x * 2 + core, y_hi * 4 + z)


def turn_tile(source, target, i, tiles):
    for j in range(tiles):
        target[i, j * TILE : (j + 1) * TILE, :] = source[j, i * TILE : (i + 1) * TILE, :].T


PARTS = 2
CUTS = (112, 96)
CHUNKS = 8
GROUPS = {
    1: ((0, 1), (7, 1)),
    3: ((1, 2), (8, 1)),
    5: ((3, 1), (9, 2)),
    6: ((4, 1), (11, 1)),
    7: ((5, 2), (12, 1)),
}
GROUP_AT = {start: at for at, start in enumerate(g[0] for gs in GROUPS.values() for g in gs)}
ROWS = 8


def recurrence_kernel(
    tile_k,
    columns_ref,
    signs_ref,
    x_ref,
    tiles_ref,
    occ_rows,
    occ_cols,
    shift_ref,
    out_ref,
    numbers_ref,
    own,
    near,
    far,
    turned,
    turned_near,
    gathered_a,
    gathered_b,
    result,
    returned,
    weights,
    kept,
    hopped_kept,
    sums,
    first,
    second,
    factors,
    load_sem,
    tiles_sem,
    sib_send,
    sib_recv,
    near_send,
    near_recv,
    far_send,
    far_recv,
    share_send,
    share_recv,
    ring_send,
    ring_recv,
    late_send,
    late_recv,
    back_send,
    back_recv,
    swap_send,
    swap_recv,
    down_send,
    down_recv,
    up_send,
    up_recv,
    free_sem,
    ready_sem,
):
    half = x_ref.shape[0]
    side = 2 * half
    quarter = side // RING
    piece = quarter // PARTS
    per_piece = side // TILE
    held = RING * per_piece
    gathered = (gathered_a, gathered_b)
    y_lo, x, core, y_hi, z = place()
    u = lax.axis_index("up")
    d = lax.axis_index("dn")
    ups = lax.axis_size("up")
    downs = lax.axis_size("dn")
    r = z + core * (x - z)
    h = y_hi + core * (y_lo - y_hi)
    sibling = device(y_lo, x, 1 - core, y_hi, z)
    near_chip = device(1 - y_lo, x, core, y_hi, z)
    far_chip = device(1 - y_lo, x, core, 1 - y_hi, z)

    def ring_peer(p):
        return device(y_lo, x + core * (p - x), core, y_hi, p + core * (z - p))

    def remote(src, dst, send, recv, to):
        return pltpu.make_async_remote_copy(
            src_ref=src, dst_ref=dst, send_sem=send, recv_sem=recv, device_id=to, device_id_type=MESH
        )

    def rows_of(p, part):
        start = (p // 2) * half + (p % 2) * piece + part * quarter
        return pl.ds(pl.multiple_of(start, 16), piece)

    starts = [(q // 2) * piece + (q % 2) * CUTS[0] for q in range(CHUNKS)]
    sizes = [CUTS[q % 2] for q in range(CHUNKS)]

    barrier = pltpu.get_barrier_semaphore()
    greeted = [sibling, near_chip, far_chip] + [ring_peer((r + k) % RING) for k in range(1, RING)]
    for to in greeted:
        pl.semaphore_signal(barrier, inc=1, device_id=to, device_id_type=MESH)
    for j in range(1, downs):
        pl.semaphore_signal(barrier, inc=1, device_id=(u, (d + j) % downs), device_id_type=MESH)
    for j in range(1, ups):
        pl.semaphore_signal(barrier, inc=1, device_id=((u + j) % ups, d), device_id_type=MESH)

    base = pl.multiple_of(core * half, half)
    my_half = pl.ds(base, half)
    loads = []
    for t in range(per_piece):
        copy = pltpu.make_async_copy(
            x_ref.at[:, pl.ds(t * TILE, TILE)], own.at[t, my_half], load_sem.at[t]
        )
        copy.start()
        loads.append(copy)
    first_tile = pl.multiple_of(h * held, held)
    load_tiles = pltpu.make_async_copy(tiles_ref.at[pl.ds(first_tile, held)], weights, tiles_sem)
    load_tiles.start()
    with jax.named_scope("barrier"):
        pl.semaphore_wait(barrier, len(greeted) + downs + ups - 2)
    with jax.named_scope("load"):
        for copy in loads:
            copy.wait()
        load_tiles.wait()

    own_slot = pl.ds((h * RING + r) * per_piece, per_piece)
    near_start = ((1 - h) * RING + r) * per_piece
    near_slot = pl.ds(near_start, per_piece)

    to_sibling = remote(own.at[:, my_half], own.at[:, my_half], sib_send, sib_recv, sibling)

    def to_near(q):
        rows = pl.ds(pl.multiple_of(base + starts[q], 16), sizes[q])
        return remote(own.at[:, rows], near.at[:, rows], near_send.at[q], near_recv.at[q], near_chip)

    def own_copy(block, part, k):
        p = (r + k) % RING
        return remote(
            block.at[:, rows_of(p, part)],
            gathered[part].at[own_slot],
            ring_send.at[part, k - 1],
            ring_recv.at[part, k - 1],
            ring_peer(p),
        )

    def own_out(block):
        for part in range(PARTS):
            for k in (2, 1, 3):
                own_copy(block, part, k).start()
        for part in range(PARTS):
            gathered[part][own_slot] = block[:, rows_of(r, part)]

    def half_rows(of, q):
        return pl.ds(of * half + starts[q], sizes[q])

    def forward(q):
        rows = pl.ds(pl.multiple_of(base + starts[q], 16), sizes[q])
        return remote(near.at[:, rows], far.at[:, rows], far_send.at[q], far_recv.at[q], far_chip)

    def share_near(q):
        rows = half_rows(0, q)
        return remote(near.at[:, rows], near.at[:, rows], share_send.at[q], share_recv.at[q], sibling)

    def share_far(q):
        rows = half_rows(1, q)
        return remote(far.at[:, rows], far.at[:, rows], share_send.at[q], share_recv.at[q], sibling)

    def late_down(of, q):
        p = 2 * of + (q // 2) % 2
        part, sub = q // 4, q % 2
        at = (part * 2 + sub) * RING + (p - r) % RING
        rows = pl.ds(sub * CUTS[0], sizes[q])
        return p, remote(
            far.at[:, half_rows(of, q)],
            gathered[part].at[near_slot, rows],
            late_send.at[at],
            late_recv.at[at],
            ring_peer(p),
        )

    def pass_down(of, q):
        p, copy = late_down(of, q)

        @pl.when(p != r)
        def _():
            copy.start()

        @pl.when(p == r)
        def _():
            part, sub = q // 4, q % 2
            gathered[part][near_slot, sub * CUTS[0] : sub * CUTS[0] + sizes[q]] = far[:, half_rows(of, q)]

    def late_up(start, count, part, k):
        p = (r + k) % RING
        at = (GROUP_AT[start] * PARTS + part) * RING + k
        tiles = pl.ds(start, count)
        return remote(
            turned_near.at[tiles, rows_of(p, part)],
            gathered[part].at[pl.ds(near_start + start, count)],
            late_send.at[at],
            late_recv.at[at],
            ring_peer(p),
        )

    def pass_up(start, count):
        for i in range(start, start + count):
            turn_tile(near, turned_near, i, per_piece)
        for part in range(PARTS):
            for k in (2, 1, 3):
                late_up(start, count, part, k).start()
        tiles = pl.ds(start, count)
        for part in range(PARTS):
            gathered[part][pl.ds(near_start + start, count)] = turned_near[tiles, rows_of(r, part)]

    def arrivals_down(part):
        for k in range(1, RING):
            own_copy(own, part, k).wait_recv()
        for sub in range(2):
            for k in range(1, RING):
                at = (part * 2 + sub) * RING + k
                rows = pl.ds(sub * CUTS[0], CUTS[sub])
                remote(
                    far.at[:, rows],
                    gathered[part].at[near_slot, rows],
                    late_send.at[at],
                    late_recv.at[at],
                    ring_peer((r + k) % RING),
                ).wait_recv()

    def arrivals_up(part):
        for k in range(1, RING):
            own_copy(own, part, k).wait_recv()
        for groups in GROUPS.values():
            for start, count in groups:
                for k in range(1, RING):
                    late_up(start, count, part, k).wait_recv()

    def hop_piece(part, p, target):
        def one_tile(t, carry):
            i = p * per_piece + t
            picked = []
            values = []
            for k in range(tile_k):
                at = (h * held + i) * tile_k + k
                picked.append(gathered[part][columns_ref[at]])
                sign = (1 - 2 * signs_ref[at]).astype(jnp.float32)
                values.append((weights[i, k].astype(jnp.float32) * sign).astype(jnp.bfloat16))
            left = jnp.concatenate(picked, axis=1)
            right = jnp.concatenate(values, axis=1)
            hopped = lax.dot_general(
                left, right, (((1,), (1,)), ((), ())), preferred_element_type=jnp.float32
            )
            target[t] = hopped.astype(jnp.bfloat16)
            return carry

        lax.fori_loop(0, per_piece, one_tile, 0)

    def back_copy(part, k):
        return remote(
            result.at[part, k - 1],
            returned.at[:, rows_of(r, part)],
            back_send.at[part, k - 1],
            back_recv.at[part, k - 1],
            ring_peer((r + k) % RING),
        )

    def hop_to(part, k):
        with jax.named_scope(f"hop{part}{k}"):
            if k:
                hop_piece(part, (r + k) % RING, result.at[part, k - 1])
                back_copy(part, k).start()
            else:
                hop_piece(part, r, returned.at[:, rows_of(r, part)])

    order = (2, 1, 3, 0)

    def sum_down(use, j):
        return remote(
            first.at[use, d], first.at[use, d], down_send.at[use, j], down_recv.at[use, j], (u, (d + j) % downs)
        )

    def sum_up(use, j):
        return remote(
            second.at[use, u], second.at[use, u], up_send.at[use, j], up_recv.at[use, j], ((u + j) % ups, d)
        )

    def sum_start(use):
        first[use, d] = sums[...]
        for j in range(1, downs):
            sum_down(use, j).start()

    def sum_middle(use):
        for j in range(1, downs):
            sum_down(use, j).wait()
        total = first[use, 0]
        for j in range(1, downs):
            total = total + first[use, j]
        second[use, u] = total
        for j in range(1, ups):
            sum_up(use, j).start()

    def sum_end(use):
        for j in range(1, ups):
            sum_up(use, j).wait()
        total = second[use, 0]
        for j in range(1, ups):
            total = total + second[use, j]
        parts = [total[ROWS * i : ROWS * (i + 1)] for i in range(3)]
        return [jnp.sum(jnp.sum(part, axis=0, keepdims=True), axis=1, keepdims=True) for part in parts]

    def keep_factor(row, value):
        factors[row : row + 1, :] = jnp.broadcast_to(value, (1, TILE))

    def first_numbers():
        total, cross, square = sum_end(0)
        shift = shift_ref[0:1, 0:1]
        scale = 1.0 / jnp.maximum(jnp.sqrt(total), 1.0)
        alpha = scale * scale * (cross + shift * total)
        delta = alpha - shift
        residual = scale * scale * (square - 2.0 * delta * cross + delta * delta * total)
        beta = jnp.sqrt(jnp.maximum(residual, 1.0))
        keep_factor(0, delta)
        keep_factor(1, scale / beta)
        keep_factor(2, beta * scale)
        keep_factor(3, alpha)
        keep_factor(4, beta)

    def last_numbers():
        total, cross, square = sum_end(1)
        shift = shift_ref[0:1, 0:1]
        alpha = cross + shift * total
        delta = alpha - shift
        residual = square - 2.0 * delta * cross + delta * delta * total
        beta = jnp.sqrt(jnp.maximum(residual, 1.0))
        keep_factor(5, delta)
        keep_factor(6, 1.0 / beta)
        numbers_ref[...] = jnp.zeros_like(numbers_ref)
        numbers_ref[0:1, :] = factors[3:4, :]
        numbers_ref[1:2, :] = jnp.broadcast_to(alpha, (1, TILE))
        numbers_ref[2:3, :] = factors[4:5, :]
        numbers_ref[3:4, :] = jnp.broadcast_to(beta, (1, TILE))

    def swap(block, t, side_of):
        rows = pl.ds((1 - side_of) * half, half)
        return remote(
            block.at[t, rows], turned_near.at[t, rows], swap_send.at[t], swap_recv.at[t], sibling
        )

    def fold(value):
        return jnp.sum(value.reshape(-1, ROWS, TILE), axis=0)

    def each_block(side_of, block, act, waits):
        sums[...] = jnp.zeros_like(sums)

        def one_tile(t, carry):
            if waits:
                swap(block, t, side_of).wait_recv()
            for a in range(RING):
                rows = slice(side_of * half + a * piece, side_of * half + (a + 1) * piece)
                mine = slice(a * piece, (a + 1) * piece)
                count = jnp.dot(occ_rows[mine, :], occ_cols[t], preferred_element_type=jnp.float32)
                offset = coupling * count - shift_ref[0:1, :]
                hopped = block[t, rows].astype(jnp.float32) + turned_near[t, rows].astype(jnp.float32)
                found = act(t, rows, mine, offset, hopped)
                if found is not None:
                    for i, value in enumerate(found):
                        sums[ROWS * i : ROWS * (i + 1), :] += fold(value)
            return carry

        lax.fori_loop(0, per_piece, one_tile, 0)

    def first_work(t, rows, mine, offset, hopped):
        start = own[t, rows]
        kept[t, mine] = start
        hopped_kept[t, mine] = hopped.astype(jnp.bfloat16)
        start = start.astype(jnp.float32)
        work = hopped + offset * start
        own[t, rows] = work.astype(jnp.bfloat16)
        return start * start, work * start, work * work

    def second_work(t, rows, mine, offset, hopped):
        delta, gain, push = factors[0:1, :], factors[1:2, :], factors[2:3, :]
        start = kept[t, mine].astype(jnp.float32)
        before = own[t, rows].astype(jnp.float32) - delta * start
        vector = gain * before
        held_hop = hopped_kept[t, mine].astype(jnp.float32)
        work = gain * (hopped - delta * held_hop + offset * before) - push * start
        return vector, work

    def second_sums(t, rows, mine, offset, hopped):
        vector, work = second_work(t, rows, mine, offset, hopped)
        return vector * vector, work * vector, work * work

    def finish(t, rows, mine, offset, hopped):
        vector, work = second_work(t, rows, mine, offset, hopped)
        final = (work - factors[5:6, :] * vector) * factors[6:7, :]
        hopped_kept[t, mine] = final.astype(jnp.bfloat16)

    def one_step(step, carry):
        to_sibling.start()
        for q in range(CHUNKS):
            to_near(q).start()
        with jax.named_scope("sibling"):
            to_sibling.wait_recv()

        @pl.when(core == 0)
        def _():
            own_out(own)

        @pl.when(core == 1)
        def _():
            with jax.named_scope("turn_own"):
                for i in range(per_piece):
                    turn_tile(own, turned, i, per_piece)
            own_out(turned)

        @pl.when(step == 1)
        def _():
            sum_middle(0)

        @pl.when(core == 0)
        def _():
            for q in range(CHUNKS + 1):
                if q < CHUNKS:
                    with jax.named_scope(f"near{q}"):
                        to_near(q).wait_recv()
                    forward(q).start()
                    share_near(q).start()
                if q >= 1:
                    with jax.named_scope(f"far{q - 1}"):
                        forward(q - 1).wait_recv()
                    pass_down(0, q - 1)
                    with jax.named_scope(f"share{q - 1}"):
                        share_far(q - 1).wait_recv()
                    pass_down(1, q - 1)
                if q == 5:
                    with jax.named_scope("arrive0"):
                        arrivals_down(0)
                if q >= 5:
                    hop_to(0, order[q - 5])
            with jax.named_scope("arrive1"):
                arrivals_down(1)

        @pl.when(core == 1)
        def _():
            for q in range(CHUNKS + 1):
                if q < CHUNKS:
                    with jax.named_scope(f"near{q}"):
                        to_near(q).wait_recv()
                    forward(q).start()
                if q >= 1:
                    with jax.named_scope(f"far{q - 1}"):
                        forward(q - 1).wait_recv()
                    share_far(q - 1).start()
                if q < CHUNKS:
                    with jax.named_scope(f"share{q}"):
                        share_near(q).wait_recv()
                    for start, count in GROUPS.get(q, ()):
                        pass_up(start, count)
            with jax.named_scope("arrive0"):
                arrivals_up(0)
            for k in order:
                hop_to(0, k)
            with jax.named_scope("arrive1"):
                arrivals_up(1)

        for k in order:
            hop_to(1, k)

        @pl.when(step == 1)
        def _():
            first_numbers()

        for part in range(PARTS):
            for k in range(1, RING):
                own_copy(own, part, k).wait_send()
        to_sibling.wait_send()
        for q in range(CHUNKS):
            to_near(q).wait_send()
            forward(q).wait_send()

        @pl.when(core == 0)
        def _():
            for q in range(CHUNKS):
                share_near(q).wait_send()
                for of in range(2):
                    p, copy = late_down(of, q)

                    @pl.when(p != r)
                    def _():
                        copy.wait_send()

        @pl.when(core == 1)
        def _():
            for q in range(CHUNKS):
                share_far(q).wait_send()
            for groups in GROUPS.values():
                for start, count in groups:
                    for part in range(PARTS):
                        for k in range(1, RING):
                            late_up(start, count, part, k).wait_send()

        pl.semaphore_signal(ready_sem, inc=1, device_id=sibling, device_id_type=MESH)

        @pl.when(step == 0)
        def _():
            for to in greeted:
                pl.semaphore_signal(free_sem, inc=1, device_id=to, device_id_type=MESH)

        with jax.named_scope("back"):
            for part in range(PARTS):
                for k in range(1, RING):
                    back_copy(part, k).wait()
        with jax.named_scope("ready"):
            pl.semaphore_wait(ready_sem, 1)

        def work_through(side_of, block):
            for t in range(per_piece):
                if side_of:
                    turn_tile(returned, turned, t, per_piece)
                swap(block, t, side_of).start()

            @pl.when(step == 0)
            def _():
                with jax.named_scope("work0"):
                    each_block(side_of, block, first_work, True)
                sum_start(0)

            @pl.when(step == 1)
            def _():
                with jax.named_scope("work1"):
                    each_block(side_of, block, second_sums, True)
                sum_start(1)
                with jax.named_scope("sum"):
                    sum_middle(1)
                    last_numbers()
                with jax.named_scope("finish"):
                    each_block(side_of, block, finish, False)

            for t in range(per_piece):
                swap(block, t, side_of).wait_send()

        @pl.when(core == 0)
        def _():
            work_through(0, returned)

        @pl.when(core == 1)
        def _():
            work_through(1, turned)

        @pl.when(step == 0)
        def _():
            with jax.named_scope("free"):
                pl.semaphore_wait(free_sem, len(greeted))

        return carry

    lax.fori_loop(0, STEPS, one_step, 0)
    with jax.named_scope("out"):
        stores = []
        for t in range(per_piece):
            copy = pltpu.make_async_copy(
                hopped_kept.at[t], out_ref.at[:, pl.ds(t * TILE, TILE)], load_sem.at[t]
            )
            copy.start()
            stores.append(copy)
        for copy in stores:
            copy.wait()


def body(start_vector, hop_tiles, tile_columns, tile_signs, occupation):
    half, side = start_vector.shape
    tile_k = hop_tiles.shape[1]
    sites, dets = occupation.shape
    per_piece = side // TILE
    held = RING * per_piece
    quarter = side // RING
    piece = quarter // PARTS
    ups = lax.axis_size("up")
    downs = lax.axis_size("dn")
    occupied = occupation.astype(jnp.bfloat16)
    row_start = lax.axis_index("up") * half
    col_start = lax.axis_index("dn") * side
    rows = lax.dynamic_slice_in_dim(occupied, row_start, half, 1).T
    cols = lax.dynamic_slice_in_dim(occupied, col_start, side, 1)
    rows = jnp.pad(rows, ((0, 0), (0, TILE - sites)))
    cols = jnp.pad(cols, ((0, TILE - sites), (0, 0))).reshape(TILE, per_piece, TILE).transpose(1, 0, 2)
    share = jnp.sum(occupation, axis=1).astype(jnp.float32) / dets
    shift = jnp.broadcast_to(coupling * jnp.sum(share * share), (ROWS, TILE))

    anywhere = pl.BlockSpec(memory_space=pl.ANY)
    scalars = pl.BlockSpec(memory_space=pltpu.SMEM)
    vmem = pl.BlockSpec(memory_space=pltpu.VMEM)
    block = pltpu.VMEM((per_piece, side, TILE), jnp.bfloat16)
    half_block = pltpu.VMEM((per_piece, half, TILE), jnp.bfloat16)
    dma = pltpu.SemaphoreType.DMA
    final, numbers = pl.pallas_call(
        functools.partial(recurrence_kernel, tile_k),
        in_specs=[scalars, scalars, anywhere, anywhere, vmem, vmem, vmem],
        out_specs=[anywhere, vmem],
        out_shape=[
            jax.ShapeDtypeStruct(start_vector.shape, jnp.bfloat16),
            jax.ShapeDtypeStruct((ROWS, TILE), jnp.float32),
        ],
        scratch_shapes=[
            block,
            block,
            block,
            block,
            block,
            pltpu.VMEM((2 * held, piece, TILE), jnp.bfloat16),
            pltpu.VMEM((2 * held, piece, TILE), jnp.bfloat16),
            pltpu.VMEM((PARTS, RING - 1, per_piece, piece, TILE), jnp.bfloat16),
            block,
            pltpu.VMEM((held, tile_k, TILE, TILE), jnp.bfloat16),
            half_block,
            half_block,
            pltpu.VMEM((3 * ROWS, TILE), jnp.float32),
            pltpu.VMEM((STEPS, downs, 3 * ROWS, TILE), jnp.float32),
            pltpu.VMEM((STEPS, ups, 3 * ROWS, TILE), jnp.float32),
            pltpu.VMEM((ROWS, TILE), jnp.float32),
            dma((per_piece,)),
            dma,
            dma,
            dma,
            dma((CHUNKS,)),
            dma((CHUNKS,)),
            dma((CHUNKS,)),
            dma((CHUNKS,)),
            dma((CHUNKS,)),
            dma((CHUNKS,)),
            dma((PARTS, RING - 1)),
            dma((PARTS, RING - 1)),
            dma((len(GROUP_AT) * PARTS * RING,)),
            dma((len(GROUP_AT) * PARTS * RING,)),
            dma((PARTS, RING - 1)),
            dma((PARTS, RING - 1)),
            dma((per_piece,)),
            dma((per_piece,)),
            dma((STEPS, downs)),
            dma((STEPS, downs)),
            dma((STEPS, ups)),
            dma((STEPS, ups)),
            pltpu.SemaphoreType.REGULAR,
            pltpu.SemaphoreType.REGULAR,
        ],
        compiler_params=pltpu.CompilerParams(
            collective_id=0, has_side_effects=True, vmem_limit_bytes=67043328
        ),
        name="recurrence",
    )(tile_columns.reshape(-1), tile_signs.reshape(-1), start_vector, hop_tiles, rows, cols, shift)
    return (final, numbers[0:2, 0], numbers[2:4, 0])


def solution(mesh):
    placed = (P("up", "dn"), P(), P(), P(), P())
    return jax.shard_map(
        body, mesh=mesh, in_specs=placed, out_specs=(P("up", "dn"), P(), P()), check_vma=False
    )
```

time: 328 us -> 292 us (0.89)
  other arithmetic: 24.4 us -> 5.17 us
  matrix products: 8.89 us -> 0 us
  Pallas kernels: 277 us -> 269 us
  between operations: 7.12 us -> 1.34 us
  local copies, waits for them, and re-layouts: 10.4 us -> 16 us
    convert_element_type x2 -> x1, other arithmetic: 13.6 us -> 3.19 us  [body(): occupied = occupation.astype(jnp.bfloat16)]
    dot_general x1 -> x0, matrix products: 8.89 us -> none  [body(): jnp.einsum('sa,sb->ab', occ_rows, occ_cols, preferred_element_type=jnp.fl...]
    reduce_sum x1 -> x2, other arithmetic: 9.6 us -> 1.98 us  [the longest x1 1.38 us: body(): share = jnp.sum(occupation, axis=1).astype(jnp.float32) / dets]
    pallas_call x4 -> x1, Pallas kernels: 277 us -> 269 us  [body(): pl.pallas_call(functools.partial(recurrence_kernel, tile_k), in_specs=[sc...]
    unnamed x8, local copies, waits for them, and re-layouts: 2.76 us -> 8.87 us
where the time goes in v3:
time: 292 us
  Pallas kernels  269 us (92%)
  local copies, waits for them, and re-layouts  16 us (5%)
  other arithmetic  5.17 us (2%)
    pallas_call x1, Pallas kernels, body(): pl.pallas_call(functools.partial(recurrence_kernel, tile_k), in_specs=[sc...  269 us
    unnamed x8, local copies, waits for them, and re-layouts  8.87 us

profile of v3, /device:TPU:1, one launch (start us, length us, event | category | flops | bytes accessed | tf_op | source)
XLA Modules:
  0.0 291.8 jit_solution(6121471499097390256)
XLA Ops:
  0.6 5.1 %copy.11 = s32[16,13312]{0,1:T(8,128)} copy(s32[16,13312]{1,0:T(8,128)} %param.9) | data formatting | bytes 1703936 | tf_op args[4]
  5.8 3.2 %convert_element_type.10 = bf16[16,13312]{0,1:T(8,128)(2,1)S(1)} convert(s32[16,13312]{0,1:T(8,128)} %copy.11) | non-fusion elementwise | flops 212992 | bytes 1277952 | tf_op jit(solution)/shard_map/convert_element_type | solution.py:615
  9.0 0.0 copy-start
  9.0 0.0 copy-start.1
  9.0 0.8 pad.9
  9.9 2.0 copy.12
  11.9 0.7 pad.8.occ_rows
  12.6 0.0 copy-done
  12.6 0.1 copy.9
  12.7 0.8 reshape.15.columns_ref
  13.5 0.0 copy-done.1
  13.5 0.1 copy.10
  13.6 0.8 reshape.16.signs_ref
  14.4 1.4 reduce_sum.18
  15.7 0.6 multiply_reduce_fusion
  17.0 0.6 broadcast_in_dim.3.shift_ref
  17.6 269.2 %recurrence.1 = (bf16[832,1664]{1,0:T(8,128)(2,1)}, f32[8,128]{1,0:T(8,128)}) custom-call(s32[520]{0:T(1024)} %reshape.15.columns_ref, s32[520]{0:T(1024)} %reshape.16.signs_ref, bf16[832,1664]{1,0:T(8,128)(2,1)} %x_ref.1, bf16[104,5,128,128]{3,2,1,0:T(8,128)(2,1)} %tiles_ref.1, bf16[832,128]{1,0:T(8,128)(2,1)} %pad.8.occ_rows, ...), custom_call_target="tpu_custom_call" | custom-call | tf_op jit(solution)/shard_map/recurrence/pallas_call | solution.py:631
  286.8 1.4 slice_reduce_fusion
  288.2 3.5 %copy.14 = bf16[832,1664]{1,0:T(8,128)(2,1)} copy(bf16[832,1664]{1,0:T(8,128)(2,1)} %get-tuple-element.12) | data formatting | bytes 5537792
  (2 shorter events, 0.1 us)
Async XLA Ops:
  9.0 3.6 %copy-start = (s32[104,5]{0,1:T(8,128)S(1)}, s32[104,5]{0,1:T(8,128)}, u32[]{:S(2)}) copy-start(s32[104,5]{0,1:T(8,128)} %param.7) | copy-start | bytes 6244
  9.0 4.5 %copy-start.1 = (s32[104,5]{0,1:T(8,128)S(1)}, s32[104,5]{0,1:T(8,128)}, u32[]{:S(2)}) copy-start(s32[104,5]{0,1:T(8,128)} %param.8) | copy-start | bytes 6244

commit v4 on v0

v4 whole, which is shorter than its diff:
```python
import functools

import jax
import jax.numpy as jnp
from jax import lax
from jax.experimental import pallas as pl
from jax.experimental.pallas import tpu as pltpu
from jax.sharding import PartitionSpec as P

STEPS = 2
RING = 4
TILE = 128
MESH = pl.DeviceIdType.MESH

coupling = 4.0


def place():
    u = lax.axis_index("up")
    d = lax.axis_index("dn")
    return u // 8, (u // 2) % 4, u % 2, d // 4, d % 4


def device(y_lo, x, core, y_hi, z):
    return (y_lo * 8 + x * 2 + core, y_hi * 4 + z)


PARTS = 2
CUTS = (112, 96)
CHUNKS = 8
LENT = 64
WIDTH = 7
TILES_OF = ((0, 7), (7, 6))
GROUPS = (
    {1: (0, 1), 3: (1, 2), 5: (3, 1), 6: (4, 1), 7: (5, 2)},
    {1: (7, 1), 3: (8, 1), 5: (9, 2), 6: (11, 1), 7: (12, 1)},
)
COUNT = 5
ROWS = 8
ORDER = (2, 1, 3, 0)


def recurrence_kernel(
    tile_k,
    columns_ref,
    signs_ref,
    x_ref,
    tiles_ref,
    occ_ref,
    out_ref,
    numbers_ref,
    own,
    near,
    far,
    turned,
    turned_near,
    gathered_a,
    gathered_b,
    result,
    back_down,
    back_up,
    hopped_up,
    weights,
    kept,
    hopped_kept,
    occ_all,
    occ_rows,
    occ_cols,
    shift_ref,
    sums,
    first,
    second,
    factors,
    load_sem,
    tiles_sem,
    occ_sem,
    near_send,
    near_recv,
    far_send,
    far_recv,
    lend_send,
    lend_recv,
    own_down_send,
    own_down_recv,
    own_up_send,
    own_up_recv,
    late_down_send,
    late_down_recv,
    late_up_send,
    late_up_recv,
    back_down_send,
    back_down_recv,
    back_up_send,
    back_up_recv,
    down_send,
    down_recv,
    up_send,
    up_recv,
    free_sem,
):
    half, side = x_ref.shape
    sites, dets = occ_ref.shape
    quarter = side // RING
    piece = quarter // PARTS
    per_piece = side // TILE
    held = RING * per_piece
    gathered = (gathered_a, gathered_b)
    y_lo, x, core, y_hi, z = place()
    u = lax.axis_index("up")
    d = lax.axis_index("dn")
    ups = lax.axis_size("up")
    downs = lax.axis_size("dn")
    sibling = device(y_lo, x, 1 - core, y_hi, z)
    near_chip = device(1 - y_lo, x, core, y_hi, z)
    far_chip = device(1 - y_lo, x, core, 1 - y_hi, z)

    def remote(src, dst, send, recv, to):
        return pltpu.make_async_remote_copy(
            src_ref=src, dst_ref=dst, send_sem=send, recv_sem=recv, device_id=to, device_id_type=MESH
        )

    starts = [(q // 2) * piece + (q % 2) * CUTS[0] for q in range(CHUNKS)]
    sizes = [CUTS[q % 2] for q in range(CHUNKS)]

    def chip_rows(p, part):
        start = (p // 2) * half + (p % 2) * piece + part * quarter
        return pl.ds(pl.multiple_of(start, 16), piece)

    def half_rows(p, part):
        start = (p % 2) * piece + part * quarter
        return pl.ds(pl.multiple_of(start, 16), piece)

    barrier = pltpu.get_barrier_semaphore()
    partners = [sibling, near_chip, far_chip]
    for k in range(1, RING):
        for c in range(2):
            partners.append(device(y_lo, x, c, y_hi, (z + k) % RING))
            partners.append(device(y_lo, (x + k) % RING, c, y_hi, z))
    others = [device(y_lo, x, core, 1 - y_hi, (z + k) % RING) for k in range(RING)]
    others += [device(1 - y_lo, (x + k) % RING, core, y_hi, z) for k in range(1, RING)]
    others += [device(1 - y_lo, (x + k) % RING, 1 - core, y_hi, z) for k in range(RING)]
    for to in partners + others:
        pl.semaphore_signal(barrier, inc=1, device_id=to, device_id_type=MESH)

    loads = []
    for t in range(per_piece):
        copy = pltpu.make_async_copy(
            x_ref.at[:, pl.ds(t * TILE, TILE)], own.at[t, pl.ds(0, half)], load_sem.at[t]
        )
        copy.start()
        loads.append(copy)
    hop_side = y_hi + core * (y_lo - y_hi)
    first_tile = pl.multiple_of(hop_side * held, held)
    load_tiles = pltpu.make_async_copy(tiles_ref.at[pl.ds(first_tile, held)], weights, tiles_sem)
    load_tiles.start()
    load_occ = pltpu.make_async_copy(occ_ref, occ_all, occ_sem)
    load_occ.start()
    with jax.named_scope("barrier"):
        pl.semaphore_wait(barrier, len(partners) + len(others))
    with jax.named_scope("load"):
        for copy in loads:
            copy.wait()

    down_slot = pl.ds((y_hi * RING + z) * per_piece, per_piece)
    late_down_slot = pl.ds(((1 - y_hi) * RING + z) * per_piece, per_piece)
    up_start = (y_lo * RING + x) * per_piece
    late_up_start = ((1 - y_lo) * RING + x) * per_piece

    def to_near(q):
        rows = pl.ds(starts[q], sizes[q])
        return remote(own.at[:, rows], near.at[:, rows], near_send.at[q], near_recv.at[q], near_chip)

    def forward(q):
        rows = pl.ds(starts[q], sizes[q])
        return remote(near.at[:, rows], far.at[:, rows], far_send.at[q], far_recv.at[q], far_chip)

    def lend(which):
        block = (own, near)[which]
        return remote(
            block.at[:, pl.ds(0, LENT)],
            block.at[:, pl.ds(half, LENT)],
            lend_send.at[which],
            lend_recv.at[which],
            sibling,
        )

    def own_down(p, part):
        at = part * RING + (p - z) % RING
        return remote(
            own.at[:, half_rows(p, part)],
            gathered[part].at[down_slot],
            own_down_send.at[at],
            own_down_recv.at[at],
            device(y_lo, x, 0, y_hi, p),
        )

    def late_down(p, part, sub):
        at = (part * 2 + sub) * RING + (p - z) % RING
        start = (p % 2) * piece + part * quarter + sub * CUTS[0]
        return remote(
            far.at[:, pl.ds(pl.multiple_of(start, 16), CUTS[sub])],
            gathered[part].at[late_down_slot, pl.ds(sub * CUTS[0], CUTS[sub])],
            late_down_send.at[at],
            late_down_recv.at[at],
            device(y_lo, x, 0, y_hi, p),
        )

    def own_up(c, part, k):
        p = (x + k) % RING
        tile, count = TILES_OF[c]
        at = (c * PARTS + part) * RING + k
        return remote(
            turned.at[pl.ds(0, count), chip_rows(p, part)],
            gathered[part].at[pl.ds(up_start + tile, count)],
            own_up_send.at[at],
            own_up_recv.at[at],
            device(y_lo, p, 1, y_hi, z),
        )

    def late_up(c, group, part, k):
        p = (x + k) % RING
        tile, count = group
        number = list(GROUPS[c].values()).index(group)
        at = ((c * COUNT + number) * PARTS + part) * RING + k
        return remote(
            turned_near.at[pl.ds(tile - TILES_OF[c][0], count), chip_rows(p, part)],
            gathered[part].at[pl.ds(late_up_start + tile, count)],
            late_up_send.at[at],
            late_up_recv.at[at],
            device(y_lo, p, 1, y_hi, z),
        )

    def result_down(part, k):
        at = part * RING + k
        return remote(
            result.at[part, k],
            back_down.at[:, half_rows(z, part)],
            back_down_send.at[at],
            back_down_recv.at[at],
            device(y_lo, x, z // 2, y_hi, (z + k) % RING),
        )

    def result_up(part, k, c):
        at = part * RING + k
        return remote(
            result.at[part, k, pl.ds(c * (per_piece - WIDTH), WIDTH)],
            back_up.at[:, chip_rows(x, part)],
            back_up_send.at[c, at],
            back_up_recv.at[at],
            device(y_lo, (x + k) % RING, c, y_hi, z),
        )

    def turn_tile(c, source, target, i):
        top = i * TILE - c * half
        for j in range(per_piece):
            target[i - TILES_OF[c][0], j * TILE : (j + 1) * TILE, :] = source[j, top : top + TILE, :].T

    def hop_piece(part, p, target):
        def one_tile(t, carry):
            i = p * per_piece + t
            picked = []
            values = []
            for k in range(tile_k):
                picked.append(gathered[part][columns_ref[hop_side * held + i, k]])
                sign = (1 - 2 * signs_ref[hop_side * held + i, k]).astype(jnp.float32)
                values.append((weights[i, k].astype(jnp.float32) * sign).astype(jnp.bfloat16))
            left = jnp.concatenate(picked, axis=1)
            right = jnp.concatenate(values, axis=1)
            hopped = lax.dot_general(
                left, right, (((1,), (1,)), ((), ())), preferred_element_type=jnp.float32
            )
            target[t] = hopped.astype(jnp.bfloat16)
            return carry

        lax.fori_loop(0, per_piece, one_tile, 0)

    def hop_to(c, part, k):
        with jax.named_scope(f"hop{part}{k}"):
            if c == 0:
                hop_piece(part, (z + k) % RING, result.at[part, k])
                if k:
                    result_down(part, k).start()
                else:

                    @pl.when(z // 2 == 1)
                    def _():
                        result_down(part, 0).start()

                    @pl.when(z // 2 == 0)
                    def _():
                        back_down[:, half_rows(z, part)] = result[part, 0]
            else:
                hop_piece(part, (x + k) % RING, result.at[part, k])
                result_up(part, k, 0).start()
                if k:
                    result_up(part, k, 1).start()
                else:
                    back_up[:, chip_rows(x, part)] = result[part, 0, per_piece - WIDTH :]

    def arrive(c, part):
        if c == 0:
            for k in range(1, RING):
                own_down((z + k) % RING, part).wait_recv()
                for sub in range(2):
                    late_down((z + k) % RING, part, sub).wait_recv()

            @pl.when(z // 2 == 1)
            def _():
                own_down(z, part).wait_recv()
                for sub in range(2):
                    late_down(z, part, sub).wait_recv()
        else:
            for side_of in range(2):
                for k in range(side_of, RING):
                    own_up(side_of, part, k).wait_recv()
                    for group in GROUPS[side_of].values():
                        late_up(side_of, group, part, k).wait_recv()

    def sum_down(use, j):
        return remote(
            first.at[use, d], first.at[use, d], down_send.at[use, j], down_recv.at[use, j], (u, (d + j) % downs)
        )

    def sum_up(use, j):
        return remote(
            second.at[use, u], second.at[use, u], up_send.at[use, j], up_recv.at[use, j], ((u + j) % ups, d)
        )

    def sum_start(use):
        first[use, d] = sums[...]
        for j in range(1, downs):
            sum_down(use, j).start()

    def sum_middle(use):
        for j in range(1, downs):
            sum_down(use, j).wait()
        total = first[use, 0]
        for j in range(1, downs):
            total = total + first[use, j]
        second[use, u] = total
        for j in range(1, ups):
            sum_up(use, j).start()

    def sum_end(use):
        for j in range(1, ups):
            sum_up(use, j).wait()
        total = second[use, 0]
        for j in range(1, ups):
            total = total + second[use, j]
        parts = [total[ROWS * i : ROWS * (i + 1)] for i in range(3)]
        return [jnp.sum(jnp.sum(part, axis=0, keepdims=True), axis=1, keepdims=True) for part in parts]

    def keep_factor(row, value):
        factors[row : row + 1, :] = jnp.broadcast_to(value, (1, TILE))

    def first_numbers():
        total, cross, square = sum_end(0)
        shift = shift_ref[0:1, 0:1]
        scale = 1.0 / jnp.maximum(jnp.sqrt(total), 1.0)
        alpha = scale * scale * (cross + shift * total)
        delta = alpha - shift
        residual = scale * scale * (square - 2.0 * delta * cross + delta * delta * total)
        beta = jnp.sqrt(jnp.maximum(residual, 1.0))
        keep_factor(0, delta)
        keep_factor(1, scale / beta)
        keep_factor(2, beta * scale)
        keep_factor(3, alpha)
        keep_factor(4, beta)

    def last_numbers():
        total, cross, square = sum_end(1)
        shift = shift_ref[0:1, 0:1]
        alpha = cross + shift * total
        delta = alpha - shift
        residual = square - 2.0 * delta * cross + delta * delta * total
        beta = jnp.sqrt(jnp.maximum(residual, 1.0))
        keep_factor(5, delta)
        keep_factor(6, 1.0 / beta)
        numbers_ref[...] = jnp.zeros_like(numbers_ref)
        numbers_ref[0:1, :] = factors[3:4, :]
        numbers_ref[1:2, :] = jnp.broadcast_to(alpha, (1, TILE))
        numbers_ref[2:3, :] = factors[4:5, :]
        numbers_ref[3:4, :] = jnp.broadcast_to(beta, (1, TILE))

    def prepare_diagonal():
        load_occ.wait()
        blank = jnp.zeros((TILE - sites, TILE), jnp.bfloat16)
        row_base = (y_lo * RING + x) * side
        col_base = d * side

        def one_block(j, carry):
            for base, turn, target in ((row_base, True, occ_rows), (col_base, False, occ_cols)):
                lanes = pl.ds(pl.multiple_of(base + j * TILE, TILE), TILE)
                found = occ_all[:, lanes].astype(jnp.float32).astype(jnp.bfloat16)
                filled = jnp.concatenate([found, blank], axis=0)
                target[j] = filled.T if turn else filled
            return carry

        lax.fori_loop(0, per_piece, one_block, 0)

        def add_tile(j, carry):
            return carry + occ_all[:, pl.ds(pl.multiple_of(j * TILE, TILE), TILE)]

        counts = lax.fori_loop(0, dets // TILE, add_tile, jnp.zeros((sites, TILE), jnp.int32))
        share = jnp.sum(counts.astype(jnp.float32), axis=1, keepdims=True) * (1.0 / dets)
        mean = coupling * jnp.sum(share * share, axis=0, keepdims=True)
        shift_ref[...] = jnp.broadcast_to(mean, shift_ref.shape)

    def fold(value):
        return jnp.sum(value.reshape(-1, ROWS, TILE), axis=0)

    blocks = [(a * TILE, min(TILE, half - a * TILE)) for a in range(WIDTH)]

    def each_block(c, act, count=3):
        def one_tile(t, totals):
            totals = list(totals)
            for start, size in blocks:
                rows = slice(start, start + size)
                top = c * half + start
                tops = [(top // TILE, top % TILE, min(size, TILE - top % TILE))]
                if tops[0][2] < size:
                    tops.append((top // TILE + 1, 0, size - tops[0][2]))
                left = [occ_rows[i, low : low + n, :] for i, low, n in tops]
                left = left[0] if len(left) == 1 else jnp.concatenate(left, axis=0)
                offset = jnp.dot(left, occ_cols[t], preferred_element_type=jnp.float32)
                offset = coupling * offset - shift_ref[0:1, :]
                lifted = slice(c * LENT + start, c * LENT + start + size)
                found = act(t, rows, lifted, offset)
                if found is not None:
                    totals = [total + fold(value) for total, value in zip(totals, found)]
            return tuple(totals)

        zero = jnp.zeros((ROWS, TILE), jnp.float32)
        return lax.fori_loop(0, per_piece, one_tile, (zero,) * count)

    def both_hops(t, rows, lifted):
        return back_down[t, rows].astype(jnp.float32) + hopped_up[t, lifted].astype(jnp.float32)

    def first_work(t, rows, lifted, offset):
        hopped = both_hops(t, rows, lifted)
        start = own[t, rows]
        kept[t, rows] = start
        hopped_kept[t, rows] = hopped.astype(jnp.bfloat16)
        start = start.astype(jnp.float32)
        work = hopped + offset * start
        own[t, rows] = work.astype(jnp.bfloat16)
        return start * start, work * start, work * work

    def held_vector(t, rows):
        start = kept[t, rows].astype(jnp.float32)
        return start, own[t, rows].astype(jnp.float32) - factors[0:1, :] * start

    def second_work(t, rows, lifted, offset):
        delta, gain, push = factors[0:1, :], factors[1:2, :], factors[2:3, :]
        hopped = both_hops(t, rows, lifted)
        start, before = held_vector(t, rows)
        vector = gain * before
        held_hop = hopped_kept[t, rows].astype(jnp.float32)
        work = gain * (hopped - delta * held_hop + offset * before) - push * start
        high = work.astype(jnp.bfloat16)
        near[t, rows] = high
        far[t, rows] = (work - high.astype(jnp.float32)).astype(jnp.bfloat16)
        return vector * vector, work * vector, work * work

    def finish():
        def one_tile(t, carry):
            for start, size in blocks:
                rows = slice(start, start + size)
                work = near[t, rows].astype(jnp.float32) + far[t, rows].astype(jnp.float32)
                _, before = held_vector(t, rows)
                final = (work - factors[5:6, :] * factors[1:2, :] * before) * factors[6:7, :]
                hopped_kept[t, rows] = final.astype(jnp.bfloat16)
            return carry

        lax.fori_loop(0, per_piece, one_tile, 0)

    def send_down(c, p, copy, copy_self):
        if c == 0:

            @pl.when(p != z)
            def _():
                copy.start()

            @pl.when(p == z)
            def _():
                copy_self()
        else:
            copy.start()

    def down_sent(c, p, copy):
        if c == 0:

            @pl.when(p != z)
            def _():
                copy.wait_send()
        else:
            copy.wait_send()

    def up_range(c):
        return range(c, RING)

    def one_step(c, step, carry):
        for q in range(CHUNKS):
            to_near(q).start()
        if c == 1:
            lend(0).start()
        for part in range(PARTS):
            for p in (2 * c, 2 * c + 1):

                def copy_self(p=p, part=part):
                    gathered[part][down_slot] = own[:, half_rows(p, part)]

                send_down(c, p, own_down(p, part), copy_self)
        tile, count = TILES_OF[c]
        with jax.named_scope("turn_own"):
            for i in range(tile, tile + count):
                if c == 0 and i == tile + count - 1:
                    lend(0).wait_recv()
                turn_tile(c, own, turned, i)
        for part in range(PARTS):
            for k in (2, 1, 3):
                own_up(c, part, k).start()
            if c == 0:
                own_up(c, part, 0).start()
            else:
                gathered[part][pl.ds(up_start + tile, count)] = turned[:count, chip_rows(x, part)]

        @pl.when(step == 0)
        def _():
            with jax.named_scope("diagonal"):
                prepare_diagonal()
                load_tiles.wait()

        @pl.when(step == 1)
        def _():
            sum_middle(0)

        for q in range(CHUNKS + 1):
            if q < CHUNKS:
                with jax.named_scope(f"near{q}"):
                    to_near(q).wait_recv()
                forward(q).start()
                if q == 0 and c == 1:
                    lend(1).start()
            if q >= 1:
                with jax.named_scope(f"far{q - 1}"):
                    forward(q - 1).wait_recv()
                p, part, sub = 2 * c + ((q - 1) // 2) % 2, (q - 1) // 4, (q - 1) % 2

                def copy_self(part=part, sub=sub, q=q):
                    rows = slice(starts[q - 1], starts[q - 1] + sizes[q - 1])
                    gathered[part][late_down_slot, sub * CUTS[0] : sub * CUTS[0] + CUTS[sub]] = far[:, rows]

                send_down(c, p, late_down(p, part, sub), copy_self)
            if q in GROUPS[c]:
                group = GROUPS[c][q]
                for i in range(group[0], group[0] + group[1]):
                    if c == 0 and i == TILES_OF[0][1] - 1:
                        lend(1).wait_recv()
                    turn_tile(c, near, turned_near, i)
                for part in range(PARTS):
                    for k in (2, 1, 3):
                        late_up(c, group, part, k).start()
                    if c == 0:
                        late_up(c, group, part, 0).start()
                    else:
                        gathered[part][pl.ds(late_up_start + group[0], group[1])] = turned_near[
                            group[0] - tile : group[0] - tile + group[1], chip_rows(x, part)
                        ]
            if c == 0 and q == 5:
                with jax.named_scope("arrive0"):
                    arrive(c, 0)
            if c == 0 and q >= 5:
                hop_to(c, 0, ORDER[q - 5])
        if c == 1:
            with jax.named_scope("arrive0"):
                arrive(c, 0)
            for k in ORDER:
                hop_to(c, 0, k)
        with jax.named_scope("arrive1"):
            arrive(c, 1)
        for k in ORDER:
            hop_to(c, 1, k)

        @pl.when(step == 1)
        def _():
            first_numbers()

        for q in range(CHUNKS):
            to_near(q).wait_send()
            forward(q).wait_send()
        if c == 1:
            lend(0).wait_send()
            lend(1).wait_send()
        for part in range(PARTS):
            for p in (2 * c, 2 * c + 1):
                down_sent(c, p, own_down(p, part))
                for sub in range(2):
                    down_sent(c, p, late_down(p, part, sub))
            for k in up_range(c):
                own_up(c, part, k).wait_send()
                for group in GROUPS[c].values():
                    late_up(c, group, part, k).wait_send()

        @pl.when(step == 0)
        def _():
            for to in partners:
                pl.semaphore_signal(free_sem, inc=1, device_id=to, device_id_type=MESH)

        with jax.named_scope("back_up"):
            for part in range(PARTS):
                for k in range(c, RING):
                    result_up(part, k, c).wait_recv()
        with jax.named_scope("turn_back"):
            for t in range(per_piece):
                for i in range(WIDTH):
                    hopped_up[t, i * TILE : (i + 1) * TILE, :] = back_up[i, t * TILE : (t + 1) * TILE, :].T
        with jax.named_scope("back_down"):
            for part in range(PARTS):
                for source in (2 * c, 2 * c + 1):
                    k = (z - source) % RING
                    copy = remote(
                        result.at[part, 0],
                        back_down.at[:, half_rows(source, part)],
                        back_down_send.at[part * RING],
                        back_down_recv.at[part * RING + k],
                        sibling,
                    )
                    if c == 0:

                        @pl.when(source != z)
                        def _():
                            copy.wait_recv()
                    else:
                        copy.wait_recv()
        for part in range(PARTS):
            for k in range(RING):
                if c == 0:
                    if k:
                        result_down(part, k).wait_send()
                    else:

                        @pl.when(z // 2 == 1)
                        def _():
                            result_down(part, 0).wait_send()
                else:
                    result_up(part, k, 0).wait_send()
                    if k:
                        result_up(part, k, 1).wait_send()

        def store_sums(found):
            for i, value in enumerate(found):
                sums[ROWS * i : ROWS * (i + 1), :] = value

        @pl.when(step == 0)
        def _():
            with jax.named_scope("work0"):
                store_sums(each_block(c, first_work))
            sum_start(0)
            with jax.named_scope("free"):
                pl.semaphore_wait(free_sem, len(partners))

        @pl.when(step == 1)
        def _():
            with jax.named_scope("work1"):
                store_sums(each_block(c, second_work))
            sum_start(1)
            with jax.named_scope("sum"):
                sum_middle(1)
                last_numbers()
            with jax.named_scope("finish"):
                finish()

        return carry

    for c in range(2):

        @pl.when(core == c)
        def _(c=c):
            lax.fori_loop(0, STEPS, functools.partial(one_step, c), 0)

    with jax.named_scope("out"):
        stores = []
        for t in range(per_piece):
            copy = pltpu.make_async_copy(
                hopped_kept.at[t], out_ref.at[:, pl.ds(t * TILE, TILE)], load_sem.at[t]
            )
            copy.start()
            stores.append(copy)
        for copy in stores:
            copy.wait()


def body(start_vector, hop_tiles, tile_columns, tile_signs, occupation):
    half, side = start_vector.shape
    tile_k = hop_tiles.shape[1]
    per_piece = side // TILE
    held = RING * per_piece
    quarter = side // RING
    piece = quarter // PARTS
    ups = lax.axis_size("up")
    downs = lax.axis_size("dn")

    anywhere = pl.BlockSpec(memory_space=pl.ANY)
    scalars = pl.BlockSpec(memory_space=pltpu.SMEM)
    vmem = pl.BlockSpec(memory_space=pltpu.VMEM)
    dma = pltpu.SemaphoreType.DMA

    def bf16(*shape):
        return pltpu.VMEM(shape, jnp.bfloat16)

    def f32(*shape):
        return pltpu.VMEM(shape, jnp.float32)

    def pair(*shape):
        return [dma(shape), dma(shape)]

    final, numbers = pl.pallas_call(
        functools.partial(recurrence_kernel, tile_k),
        in_specs=[scalars, scalars, anywhere, anywhere, anywhere],
        out_specs=[anywhere, vmem],
        out_shape=[
            jax.ShapeDtypeStruct(start_vector.shape, jnp.bfloat16),
            jax.ShapeDtypeStruct((ROWS, TILE), jnp.float32),
        ],
        scratch_shapes=[
            bf16(per_piece, half + LENT, TILE),
            bf16(per_piece, half + LENT, TILE),
            bf16(per_piece, half, TILE),
            bf16(WIDTH, side, TILE),
            bf16(WIDTH, side, TILE),
            bf16(2 * held, piece, TILE),
            bf16(2 * held, piece, TILE),
            bf16(PARTS, RING, per_piece, piece, TILE),
            bf16(per_piece, half, TILE),
            bf16(WIDTH, side, TILE),
            bf16(per_piece, half + LENT, TILE),
            bf16(held, tile_k, TILE, TILE),
            bf16(per_piece, half, TILE),
            bf16(per_piece, half, TILE),
            pltpu.VMEM(occupation.shape, jnp.int32),
            bf16(per_piece, TILE, TILE),
            bf16(per_piece, TILE, TILE),
            f32(ROWS, TILE),
            f32(3 * ROWS, TILE),
            f32(STEPS, downs, 3 * ROWS, TILE),
            f32(STEPS, ups, 3 * ROWS, TILE),
            f32(ROWS, TILE),
            dma((per_piece,)),
            dma,
            dma,
            *pair(CHUNKS),
            *pair(CHUNKS),
            *pair(2),
            *pair(PARTS * RING),
            *pair(2 * PARTS * RING),
            *pair(2 * PARTS * RING),
            *pair(2 * COUNT * PARTS * RING),
            *pair(PARTS * RING),
            dma((2, PARTS * RING)),
            dma((PARTS * RING,)),
            *pair(STEPS, downs),
            *pair(STEPS, ups),
            pltpu.SemaphoreType.REGULAR,
        ],
        compiler_params=pltpu.CompilerParams(
            collective_id=0, has_side_effects=True, vmem_limit_bytes=67043328
        ),
        name="recurrence",
    )(tile_columns, tile_signs, start_vector, hop_tiles, occupation)
    return (final, numbers[0:2, 0], numbers[2:4, 0])


def solution(mesh):
    placed = (P("up", "dn"), P(), P(), P(), P())
    return jax.shard_map(
        body, mesh=mesh, in_specs=placed, out_specs=(P("up", "dn"), P(), P()), check_vma=False
    )
```

time: 633 us -> 273 us (0.43)
  blocking collectives: 298 us -> 0 us
  Pallas kernels: 97.9 us -> 265 us
  local copies, waits for them, and re-layouts: 78.1 us -> 7.75 us
  waiting for transfers between devices: 53.3 us -> 0 us
  other arithmetic: 50.9 us -> 0 us
  starting transfers between devices: 35 us -> 0 us
  between operations: 9.17 us -> 0.64 us
  matrix products: 7.5 us -> 0 us
    psum x3 -> x0, blocking collectives: 215 us -> none  [the longest x2 129 us: body(): lax.psum((jnp.sum(work * vector), jnp.sum(work * work)), ('up', 'dn'))]
    pallas_call x4 -> x1, Pallas kernels: 97.9 us -> 265 us  [body(): pl.pallas_call(functools.partial(recurrence_kernel, tile_k), in_specs=[sc...]
    all_to_all x2 -> x0, blocking collectives: 83.6 us -> none  [body(): up = lax.all_to_all(up, 'up', 0, 0, tiled=True)]
    all_to_all x6 -> x0, waiting for transfers between devices: 53.3 us -> none  [the longest x2 30.2 us: body(): up = lax.all_to_all(up, 'up', 0, 0, tiled=True)]
    all_to_all x6 -> x0, starting transfers between devices: 35 us -> none  [the longest x4 25.5 us: body(): down = lax.all_to_all(down, 'dn', 0, 0, tiled=True)]
    transpose x4 -> x0, local copies, waits for them, and re-layouts: 32 us -> none  [the longest x1 22.8 us: body(): stacked = signed.transpose(0, 1, 3, 2).reshape(tiles, tile_k * tile, tile)]
    reshape x7 -> x0, local copies, waits for them, and re-layouts: 26.3 us -> none  [the longest x4 13.7 us: hop_blocks(): return hopped.reshape(rows, parts, width).transpose(1, 0, 2)]
    convert_element_type x5 -> x0, other arithmetic: 21.4 us -> none  [the longest x1 7.94 us: body(): rounded = start_vector if iteration == 0 else vector.astype(jnp.bfloat16)]
  transfers between devices with their start and end apart: 6 -> 0, of which waited for: 3 -> 0; matrix products, arithmetic and copies ran while one was open for 15% -> 0% of each run, Pallas kernels for 16% -> 0%
where the time goes in v4:
time: 273 us
  Pallas kernels  265 us (97%)
  local copies, waits for them, and re-layouts  7.75 us (3%)
    pallas_call x1, Pallas kernels, body(): pl.pallas_call(functools.partial(recurrence_kernel, tile_k), in_specs=[sc...  265 us
    unnamed x3, local copies, waits for them, and re-layouts  6.34 us

profile of v4, /device:TPU:1, one launch (start us, length us, event | category | flops | bytes accessed | tf_op | source)
XLA Modules:
  0.0 273.1 jit_solution(15674702918018210329)
XLA Ops:
  0.6 1.4 copy.10.columns_ref
  2.0 1.4 copy.11.signs_ref
  3.5 264.7 %recurrence.1 = (bf16[832,1664]{1,0:T(8,128)(2,1)}, f32[8,128]{1,0:T(8,128)}) custom-call(s32[104,5]{1,0:T(8,128)} %copy.10.columns_ref, s32[104,5]{1,0:T(8,128)} %copy.11.signs_ref, bf16[832,1664]{1,0:T(8,128)(2,1)} %x_ref.1, bf16[104,5,128,128]{3,2,1,0:T(8,128)(2,1)} %tiles_ref.1, s32[16,13312]{1,0:T(8,128)} %occ_ref.1), custom_call_target="tpu_custom_call" | custom-call | tf_op jit(solution)/shard_map/recurrence/pallas_call | solution.py:718
  268.1 1.4 slice_reduce_fusion
  269.6 3.5 %copy.13 = bf16[832,1664]{1,0:T(8,128)(2,1)} copy(bf16[832,1664]{1,0:T(8,128)(2,1)} %get-tuple-element.12) | data formatting | bytes 5537792

commit v5 on v4

--- a/solution.py
+++ b/solution.py
@@ -37,13 +37,13 @@
 )
 COUNT = 5
 ROWS = 8
+GROUP = 2
 ORDER = (2, 1, 3, 0)
 
 
 def recurrence_kernel(
     tile_k,
-    columns_ref,
-    signs_ref,
+    lists_ref,
     x_ref,
     tiles_ref,
     occ_ref,
@@ -256,23 +256,23 @@
             target[i - TILES_OF[c][0], j * TILE : (j + 1) * TILE, :] = source[j, top : top + TILE, :].T
 
     def hop_piece(part, p, target):
-        def one_tile(t, carry):
+        def one_tile(t):
             i = p * per_piece + t
-            picked = []
-            values = []
-            for k in range(tile_k):
-                picked.append(gathered[part][columns_ref[hop_side * held + i, k]])
-                sign = (1 - 2 * signs_ref[hop_side * held + i, k]).astype(jnp.float32)
-                values.append((weights[i, k].astype(jnp.float32) * sign).astype(jnp.bfloat16))
+            picked = [gathered[part][lists_ref[hop_side * held + i, k]] for k in range(tile_k)]
+            values = [weights[i, k] for k in range(tile_k)]
             left = jnp.concatenate(picked, axis=1)
-            right = jnp.concatenate(values, axis=1)
-            hopped = lax.dot_general(
-                left, right, (((1,), (1,)), ((), ())), preferred_element_type=jnp.float32
-            )
-            target[t] = hopped.astype(jnp.bfloat16)
+            right = jnp.concatenate(values, axis=0)
+            return jnp.dot(left, right, preferred_element_type=jnp.float32).astype(jnp.bfloat16)
+
+        def some_tiles(j, carry):
+            found = [one_tile(j * GROUP + n) for n in range(GROUP)]
+            for n in range(GROUP):
+                target[j * GROUP + n] = found[n]
             return carry
 
-        lax.fori_loop(0, per_piece, one_tile, 0)
+        lax.fori_loop(0, per_piece // GROUP, some_tiles, 0)
+        for t in range(per_piece // GROUP * GROUP, per_piece):
+            target[t] = one_tile(t)
 
     def hop_to(c, part, k):
         with jax.named_scope(f"hop{part}{k}"):
@@ -315,6 +315,17 @@
                     own_up(side_of, part, k).wait_recv()
                     for group in GROUPS[side_of].values():
                         late_up(side_of, group, part, k).wait_recv()
+
+    def prepare_tiles():
+        load_tiles.wait()
+
+        def one_row(i, carry):
+            for k in range(tile_k):
+                sign = (1 - 2 * lists_ref[2 * held + hop_side * held + i, k]).astype(jnp.float32)
+                weights[i, k] = (weights[i, k].astype(jnp.float32) * sign).astype(jnp.bfloat16).T
+            return carry
+
+        lax.fori_loop(0, held, one_row, 0)
 
     def sum_down(use, j):
         return remote(
@@ -529,7 +540,8 @@
         def _():
             with jax.named_scope("diagonal"):
                 prepare_diagonal()
-                load_tiles.wait()
+            with jax.named_scope("tiles"):
+                prepare_tiles()
 
         @pl.when(step == 1)
         def _():
@@ -717,7 +729,7 @@
 
     final, numbers = pl.pallas_call(
         functools.partial(recurrence_kernel, tile_k),
-        in_specs=[scalars, scalars, anywhere, anywhere, anywhere],
+        in_specs=[scalars, anywhere, anywhere, anywhere],
         out_specs=[anywhere, vmem],
         out_shape=[
             jax.ShapeDtypeStruct(start_vector.shape, jnp.bfloat16),
@@ -767,7 +779,7 @@
             collective_id=0, has_side_effects=True, vmem_limit_bytes=67043328
         ),
         name="recurrence",
-    )(tile_columns, tile_signs, start_vector, hop_tiles, occupation)
+    )(jnp.concatenate([tile_columns, tile_signs], axis=0), start_vector, hop_tiles, occupation)
     return (final, numbers[0:2, 0], numbers[2:4, 0])
 
 

time: 273 us -> 263 us (0.963)
  Pallas kernels: 265 us -> 256 us
    pallas_call x1, Pallas kernels: 265 us -> 256 us  [body(): pl.pallas_call(functools.partial(recurrence_kernel, tile_k), in_specs=[sc...]
    unnamed x3 -> x1, local copies, waits for them, and re-layouts: 6.34 us -> 3.52 us
where the time goes in v5:
time: 263 us
  Pallas kernels  256 us (97%)
  local copies, waits for them, and re-layouts  5.72 us (2%)
    pallas_call x1, Pallas kernels, body(): pl.pallas_call(functools.partial(recurrence_kernel, tile_k), in_specs=[sc...  256 us

profile of v5, /device:TPU:1, one launch (start us, length us, event | category | flops | bytes accessed | tf_op | source)
XLA Modules:
  0.0 262.8 jit_solution(8008978043368176543)
XLA Ops:
  0.6 0.8 pad_add_fusion
  1.4 0.8 copy.12.lists_ref
  2.2 255.7 %recurrence.1 = (bf16[832,1664]{1,0:T(8,128)(2,1)}, f32[8,128]{1,0:T(8,128)}) custom-call(s32[208,5]{1,0:T(8,128)} %copy.12.lists_ref, bf16[832,1664]{1,0:T(8,128)(2,1)} %x_ref.1, bf16[104,5,128,128]{3,2,1,0:T(8,128)(2,1)} %tiles_ref.1, s32[16,13312]{1,0:T(8,128)} %occ_ref.1), custom_call_target="tpu_custom_call" | custom-call | tf_op jit(solution)/shard_map/recurrence/pallas_call | solution.py:730
  257.9 1.4 slice_reduce_fusion
  259.3 3.5 %copy.14 = bf16[832,1664]{1,0:T(8,128)(2,1)} copy(bf16[832,1664]{1,0:T(8,128)(2,1)} %get-tuple-element.12) | data formatting | bytes 5537792

commit v6 on v5

--- a/solution.py
+++ b/solution.py
@@ -38,6 +38,7 @@
 COUNT = 5
 ROWS = 8
 GROUP = 2
+EARLY = 5
 ORDER = (2, 1, 3, 0)
 
 
@@ -422,8 +423,9 @@
 
     blocks = [(a * TILE, min(TILE, half - a * TILE)) for a in range(WIDTH)]
 
-    def each_block(c, act, count=3):
-        def one_tile(t, totals):
+    def each_block(c, act, late, count=3):
+        def one_tile(j, totals):
+            t = 3 + j + 2 * (j // 4) if late else j + 4 * (j // 3)
             totals = list(totals)
             for start, size in blocks:
                 rows = slice(start, start + size)
@@ -442,7 +444,7 @@
             return tuple(totals)
 
         zero = jnp.zeros((ROWS, TILE), jnp.float32)
-        return lax.fori_loop(0, per_piece, one_tile, (zero,) * count)
+        return lax.fori_loop(0, per_piece - EARLY if late else EARLY, one_tile, (zero,) * count)
 
     def both_hops(t, rows, lifted):
         return back_down[t, rows].astype(jnp.float32) + hopped_up[t, lifted].astype(jnp.float32)
@@ -473,6 +475,11 @@
         far[t, rows] = (work - high.astype(jnp.float32)).astype(jnp.bfloat16)
         return vector * vector, work * vector, work * work
 
+    def store(t):
+        return pltpu.make_async_copy(
+            hopped_kept.at[t], out_ref.at[:, pl.ds(pl.multiple_of(t * TILE, TILE), TILE)], load_sem.at[t]
+        )
+
     def finish():
         def one_tile(t, carry):
             for start, size in blocks:
@@ -481,6 +488,7 @@
                 _, before = held_vector(t, rows)
                 final = (work - factors[5:6, :] * factors[1:2, :] * before) * factors[6:7, :]
                 hopped_kept[t, rows] = final.astype(jnp.bfloat16)
+            store(t).start()
             return carry
 
         lax.fori_loop(0, per_piece, one_tile, 0)
@@ -619,14 +627,18 @@
             for to in partners:
                 pl.semaphore_signal(free_sem, inc=1, device_id=to, device_id_type=MESH)
 
-        with jax.named_scope("back_up"):
-            for part in range(PARTS):
+        def take_up(part):
+            with jax.named_scope("back_up"):
                 for k in range(c, RING):
                     result_up(part, k, c).wait_recv()
-        with jax.named_scope("turn_back"):
-            for t in range(per_piece):
-                for i in range(WIDTH):
-                    hopped_up[t, i * TILE : (i + 1) * TILE, :] = back_up[i, t * TILE : (t + 1) * TILE, :].T
+            with jax.named_scope("turn_back"):
+                for t in (3, 4, 5, 6, 9, 10, 11, 12) if part else (0, 1, 2, 7, 8):
+                    for i in range(WIDTH):
+                        hopped_up[t, i * TILE : (i + 1) * TILE, :] = back_up[
+                            i, t * TILE : (t + 1) * TILE, :
+                        ].T
+
+        take_up(0)
         with jax.named_scope("back_down"):
             for part in range(PARTS):
                 for source in (2 * c, 2 * c + 1):
@@ -645,6 +657,42 @@
                             copy.wait_recv()
                     else:
                         copy.wait_recv()
+        def store_sums(found, more):
+            for i, value in enumerate(found):
+                rows = slice(ROWS * i, ROWS * (i + 1))
+                sums[rows, :] = sums[rows, :] + value if more else value
+
+        @pl.when(step == 0)
+        def _():
+            with jax.named_scope("early0"):
+                store_sums(each_block(c, first_work, False), False)
+
+        @pl.when(step == 1)
+        def _():
+            with jax.named_scope("early1"):
+                store_sums(each_block(c, second_work, False), False)
+
+        take_up(1)
+
+        @pl.when(step == 0)
+        def _():
+            with jax.named_scope("work0"):
+                store_sums(each_block(c, first_work, True), True)
+            sum_start(0)
+            with jax.named_scope("free"):
+                pl.semaphore_wait(free_sem, len(partners))
+
+        @pl.when(step == 1)
+        def _():
+            with jax.named_scope("work1"):
+                store_sums(each_block(c, second_work, True), True)
+            sum_start(1)
+            with jax.named_scope("sum"):
+                sum_middle(1)
+                last_numbers()
+            with jax.named_scope("finish"):
+                finish()
+
         for part in range(PARTS):
             for k in range(RING):
                 if c == 0:
@@ -660,29 +708,6 @@
                     if k:
                         result_up(part, k, 1).wait_send()
 
-        def store_sums(found):
-            for i, value in enumerate(found):
-                sums[ROWS * i : ROWS * (i + 1), :] = value
-
-        @pl.when(step == 0)
-        def _():
-            with jax.named_scope("work0"):
-                store_sums(each_block(c, first_work))
-            sum_start(0)
-            with jax.named_scope("free"):
-                pl.semaphore_wait(free_sem, len(partners))
-
-        @pl.when(step == 1)
-        def _():
-            with jax.named_scope("work1"):
-                store_sums(each_block(c, second_work))
-            sum_start(1)
-            with jax.named_scope("sum"):
-                sum_middle(1)
-                last_numbers()
-            with jax.named_scope("finish"):
-                finish()
-
         return carry
 
     for c in range(2):
@@ -692,15 +717,8 @@
             lax.fori_loop(0, STEPS, functools.partial(one_step, c), 0)
 
     with jax.named_scope("out"):
-        stores = []
         for t in range(per_piece):
-            copy = pltpu.make_async_copy(
-                hopped_kept.at[t], out_ref.at[:, pl.ds(t * TILE, TILE)], load_sem.at[t]
-            )
-            copy.start()
-            stores.append(copy)
-        for copy in stores:
-            copy.wait()
+            store(t).wait()
 
 
 def body(start_vector, hop_tiles, tile_columns, tile_signs, occupation):

time: 263 us -> 261 us (level)
  Pallas kernels: 256 us -> 253 us
where the time goes in v6:
time: 261 us
  Pallas kernels  253 us (97%)
  local copies, waits for them, and re-layouts  5.72 us (2%)
    pallas_call x1, Pallas kernels, body(): pl.pallas_call(functools.partial(recurrence_kernel, tile_k), in_specs=[sc...  253 us

profile of v6, /device:TPU:1, one launch (start us, length us, event | category | flops | bytes accessed | tf_op | source)
XLA Modules:
  0.0 260.5 jit_solution(7753102349842531246)
XLA Ops:
  0.6 0.8 pad_add_fusion
  1.4 0.8 copy.12.lists_ref
  2.2 253.4 %recurrence.1 = (bf16[832,1664]{1,0:T(8,128)(2,1)}, f32[8,128]{1,0:T(8,128)}) custom-call(s32[208,5]{1,0:T(8,128)} %copy.12.lists_ref, bf16[832,1664]{1,0:T(8,128)(2,1)} %x_ref.1, bf16[104,5,128,128]{3,2,1,0:T(8,128)(2,1)} %tiles_ref.1, s32[16,13312]{1,0:T(8,128)} %occ_ref.1), custom_call_target="tpu_custom_call" | custom-call | tf_op jit(solution)/shard_map/recurrence/pallas_call | solution.py:748
  255.6 1.4 slice_reduce_fusion
  257.0 3.5 %copy.14 = bf16[832,1664]{1,0:T(8,128)(2,1)} copy(bf16[832,1664]{1,0:T(8,128)(2,1)} %get-tuple-element.12) | data formatting | bytes 5537792
